TPU v7x, 256 devices: a whole 4x4x8 slice. The times are simulated.
256 devices in a mesh: arcs: 16 (over x, y_hi, core), tiles: 16 (over z, y_lo).
Axes of the slice: x: 4, y: 4 (y_hi: 2, y_lo: 2; y = y_hi * 2 + y_lo), z: 8, core: 2. Of those that a mesh axis runs over, the one named last changes fastest.
Arguments:
- design: bfloat16 [24576, 8192], P('arcs', 'tiles'), may hold values from -0.09375 to 0.09375
- observations: float32 [24576], P('arcs'), may hold values from -25 to 25
- solution: float32 [8192], P('tiles'), may hold values from -6 to 6
- arc_ids: int32 [16, 1536], P('arcs'), may hold values from 0 to 3, never falling along the last dimension, each value on 1 to 768 neighbouring positions
- block_live: int32 [16, 12], P('arcs'), may hold values 0 or 1
Outputs:
- normal: float32 [8192, 8192], P('arcs', 'tiles')
- rhs: float32 [8192], P('tiles')
Inputs may be any that keep to these rules, and one draw needn't show every extreme that they name: `arc_ids`: the arcs of a group's rows never fall along its rows; an arc holds at most 768 rows and some arc exactly that many.
All inputs are finite; a program needn't handle non-finite values. No bound on the sum of `block_live` on one device may be relied on, other than what follows from the above.
Results may differ from a plain program's by a relative error of at most 0.0018.
Values may be sent and summed in bfloat16 or wider, within the bound.
No kernel may reach another device: no remote copies, remote signals or barrier semaphores. Data moves between devices by JAX's collectives and lax.ppermute only.
A program may use at most 128 MiB of HBM per device.

v0:
```python
import jax
import jax.numpy as jnp
from jax import lax
from jax.sharding import Mesh
from jax.sharding import PartitionSpec as P

ARCS_DEV = 4
TILES = ("tiles_0", "tiles_1")


prior_rows = 4.0


def gathered_by_axis(array, axes, dim):
    for axis in reversed(axes):
        array = lax.all_gather(array, axis, axis=dim, tiled=True)
    return array


def sent_to_all(array, axis):
    count = lax.axis_size(axis)
    return lax.all_to_all(
        jnp.broadcast_to(array[None], (count, *array.shape)), axis, 0, 0, tiled=True
    )


def of_everyone(array, axis):
    return sent_to_all(array, axis).sum(axis=0)


def together(arrays, axis):
    ends = [0]
    for a in arrays:
        ends.append(ends[-1] + a.size)
    total = of_everyone(jnp.concatenate([a.ravel() for a in arrays]), axis)
    return tuple((total[b:e].reshape(a.shape) for a, b, e in zip(arrays, ends, ends[1:])))


def contract_rows(left, right):
    return lax.dot_general(
        left, right, (((0,), (0,)), ((), ())), preferred_element_type=jnp.float32
    )


def local(design, observations, solution, arc_ids, block_live):
    row_count = design.shape[0]
    design_all = gathered_by_axis(design, TILES, 1)
    partial_value = jnp.dot(design.astype(jnp.float32), solution, precision=lax.Precision.HIGHEST)
    predicted = of_everyone(partial_value, TILES)
    residual = observations - predicted
    live_row = (
        jnp.broadcast_to(block_live[0][:, None], (block_live.shape[1], 128))
        .reshape(row_count)
        .astype(jnp.float32)
    )
    arc_match = (arc_ids[0][None, :] == jnp.arange(ARCS_DEV, dtype=jnp.int32)[:, None]).astype(
        jnp.float32
    )
    squares = live_row * residual * residual
    arc_squares = jnp.sum(arc_match * squares[None, :], axis=1)
    arc_counts = jnp.sum(arc_match * live_row[None, :], axis=1)
    totals = together((jnp.sum(arc_squares), jnp.sum(arc_counts)), "arcs")
    variance_all = (totals[0] + 1.0) / (totals[1] + 1.0)
    arc_weight = variance_all / (
        (arc_squares + prior_rows * variance_all) / (arc_counts + prior_rows)
    )
    row_weight = live_row * jnp.sum(arc_match * arc_weight[:, None], axis=0)
    rhs_part = lax.dot_general(
        design.astype(jnp.float32),
        row_weight * residual,
        (((0,), (0,)), ((), ())),
        precision=lax.Precision.HIGHEST,
    )
    weighted = (row_weight[:, None] * design).astype(jnp.bfloat16)
    normal = lax.psum_scatter(
        contract_rows(design_all, weighted), "arcs", scatter_dimension=0, tiled=True
    )
    rhs = of_everyone(rhs_part, "arcs")
    return (normal, rhs)


def solution(mesh):
    finer = Mesh(mesh.devices.reshape(mesh.shape["arcs"], 8, 2), ("arcs", "tiles_0", "tiles_1"))
    return jax.shard_map(
        local,
        mesh=finer,
        in_specs=(P("arcs", TILES), P("arcs"), P(TILES), P("arcs", None), P("arcs", None)),
        out_specs=(P("arcs", TILES), P(TILES)),
        check_vma=False,
    )
```

profile of v0, /device:TPU:1, one launch (start us, length us, event | category | flops | bytes accessed | tf_op | source)
XLA Modules:
  0.0 501.8 jit_solution(8807722876623244042)
XLA Ops:
  7.2 0.0 copy-start
  7.2 0.0 all-gather.3.cloned.1.call-start
  7.2 0.7 all-gather.3.cloned.1.call-update
  7.9 0.0 all-gather.5.cloned.1.call-start
  8.0 55.5 %all-gather.3.cloned.1.call-done = bf16[1536,1024]{1,0:T(8,128)(2,1)} async-done(((bf16[1536,512]{1,0:T(8,128)(2,1)}), bf16[1536,1024]{1,0:T(8,128)(2,1)}) %all-gather.3.cloned.1.call-update) | async-done | bytes 3145744 | tf_op jit(solution)/shard_map/all_gather | solution.py:16
  63.4 0.0 copy-start.1
  63.4 0.0 all-gather.5.cloned.1.call-update
  63.5 0.0 copy-done
  63.5 0.0 copy-start.3
  63.5 0.0 copy-start.4
  63.5 0.0 copy-start.2
  63.5 1.3 copy-done.1
  64.8 1.3 convolution_reduce_fusion
  66.2 0.7 broadcast_in_dim.9
  66.9 6.8 %all-to-all-start = ((f32[16,1,1536]{2,1,0:T(1,128)}), f32[16,1,1536]{2,1,0:T(1,128)S(1)}, u32[]{:S(2)}, u32[]{:S(2)}) async-start(f32[16,1,1536]{2,1,0:T(1,128)} %broadcast_in_dim.9), calls=%async_computation | async-start | bytes 196608 | tf_op jit(solution)/shard_map/all_to_all | solution.py:22
  73.7 0.0 reduce-scatter.2.cloned.1.call-start
  73.8 0.0 copy-done.3
  73.8 0.0 copy-done.4
  73.8 0.1 broadcast_bitcast_fusion
  73.9 8.0 %all-to-all-done = f32[16,1,1536]{2,1,0:T(1,128)S(1)} async-done(((f32[16,1,1536]{2,1,0:T(1,128)}), f32[16,1,1536]{2,1,0:T(1,128)S(1)}, u32[]{:S(2)}, u32[]{:S(2)}) %all-to-all-start) | async-done | bytes 98336 | tf_op jit(solution)/shard_map/all_to_all | solution.py:22
  81.9 0.1 reduce_sum.72
  82.0 0.0 copy-done.2
  82.0 0.1 multiply_multiply_fusion
  82.1 0.6 select_reduce_fusion.3
  82.7 1.4 pad_maximum_fusion
  84.1 15.8 %all_to_all.18 = f32[16,1,2]{2,1,0:T(1,128)S(1)} all-to-all(f32[16,1,2]{2,1,0:T(1,128)S(1)} %broadcast_in_dim.10), channel_id=1, replica_groups=mesh['arcs'=16,'tiles_0'=8,'tiles_1'=2] {'arcs'}, dimensions={0} | all-to-all | bytes 256 | tf_op jit(solution)/shard_map/all_to_all | solution.py:22
  99.9 0.6 fusion.2
  101.8 0.1 select_reduce_fusion.4
  101.9 0.1 fusion.1
  102.0 215.9 %all-gather.5.cloned.1.call-done = bf16[1536,8192]{1,0:T(8,128)(2,1)} async-done(((bf16[1536,1024]{1,0:T(8,128)(2,1)}), bf16[1536,8192]{1,0:T(8,128)(2,1)}) %all-gather.5.cloned.1.call-update) | async-done | bytes 25165840 | tf_op jit(solution)/shard_map/all_gather | solution.py:16
  317.9 21.7 %convolution_bitcast_fusion = f32[8192,512]{0,1:T(8,128)} fusion(bf16[1536,8192]{1,0:T(8,128)(2,1)} %all-gather.5.cloned.1.call-done, bf16[1536,512]{1,0:T(8,128)(2,1)S(1)} %copy-done.1, f32[1536]{0:T(1024)S(1)} %get-tuple-element.15), kind=kOutput, calls=%fused_computation | convolution fusion | flops 12887261184 | bytes 43522048 | tf_op jit(solution)/shard_map/dot_general | solution.py:40
  339.6 0.0 reduce-scatter.2.cloned.1.call-update
  339.7 0.7 fusion.3
  340.4 14.6 %all_to_all.19 = f32[16,1,512]{2,1,0:T(1,128)S(1)} all-to-all(f32[16,1,512]{2,1,0:T(1,128)S(1)} %broadcast_in_dim.11), channel_id=1, replica_groups=mesh['arcs'=16,'tiles_0'=8,'tiles_1'=2] {'arcs'}, dimensions={0} | all-to-all | bytes 65536 | tf_op jit(solution)/shard_map/all_to_all | solution.py:22
  355.0 0.6 reduce_sum.79
  355.7 137.1 %reduce-scatter.2.cloned.1.call-done = f32[512,512]{0,1:T(8,128)} async-done(((f32[8192,512]{0,1:T(8,128)}), f32[512,512]{0,1:T(8,128)}) %reduce-scatter.2.cloned.1.call-update) | async-done | bytes 1048592 | tf_op jit(solution)/shard_map/reduce_scatter | solution.py:75
  492.8 2.5 copy.12
  (7 shorter events, 0.1 us)
Async XLA Ops:
  7.2 56.3 %copy-start = (f32[512]{0:T(512)S(1)}, f32[512]{0:T(512)}, u32[]{:S(2)}) copy-start(f32[512]{0:T(512)} %param.7) | copy-start | bytes 6148
  7.2 56.3 %all-gather.3.cloned.1.call-start = ((), (), s32[]{:S(2)}) async-start(), calls=%async_computation.4 | async-start | bytes 4718592 | tf_op jit(solution)/shard_map/all_gather | solution.py:16
  7.9 310.0 %all-gather.5.cloned.1.call-start = ((), (), s32[]{:S(2)}) async-start(), calls=%async_computation.5 | async-start | bytes 28311552 | tf_op jit(solution)/shard_map/all_gather | solution.py:16
  63.4 1.4 copy-start.1
  63.5 10.3 %copy-start.3 = (s32[1,1536]{1,0:T(1,128)S(1)}, s32[1,1536]{1,0:T(1,128)}, u32[]{:S(2)}) copy-start(s32[1,1536]{1,0:T(1,128)} %param.8) | copy-start | bytes 18436
  63.5 10.3 %copy-start.4 = (s32[1,12]{1,0:T(1,128)S(1)}, s32[1,12]{1,0:T(1,128)}, u32[]{:S(2)}) copy-start(s32[1,12]{1,0:T(1,128)} %param.9) | copy-start | bytes 148
  63.5 18.5 %copy-start.2 = (f32[1536]{0:T(1024)S(1)}, f32[1536]{0:T(1024)}, u32[]{:S(2)}) copy-start(f32[1536]{0:T(1024)} %param.6) | copy-start | bytes 18436
  66.9 15.0 %all-to-all-start = ((f32[16,1,1536]{2,1,0:T(1,128)}), f32[16,1,1536]{2,1,0:T(1,128)S(1)}, u32[]{:S(2)}, u32[]{:S(2)}) async-start(f32[16,1,1536]{2,1,0:T(1,128)} %broadcast_in_dim.9), calls=%async_computation | async-start | bytes 196608 | tf_op jit(solution)/shard_map/all_to_all | solution.py:22
  73.7 419.1 %reduce-scatter.2.cloned.1.call-start = ((), (), s32[]{:S(2)}) async-start(), calls=%async_computation.6 | async-start | bytes 17825792 | tf_op jit(solution)/shard_map/reduce_scatter | solution.py:75
Sparse Core Ops, SparseCore 0:
  9.8 53.6 all-gather.2
  65.2 252.6 all-gather.4
  339.8 152.9 reduce-scatter.1
where the time goes:
time: 502 us
  waiting for transfers between devices  417 us (83%)
  blocking collectives  30.4 us (6%)
  matrix products  23.8 us (5%)
  between operations  15.2 us (3%)
  starting transfers between devices  6.95 us (1%)
  local copies, waits for them, and re-layouts  5.29 us (1%)
    all_gather x2, waiting for transfers between devices, gathered_by_axis(): array = lax.all_gather(array, axis, axis=dim, tiled=True)  271 us
    reduce_scatter x1, waiting for transfers between devices, local(): lax.psum_scatter(contract_rows(design_all, weighted), 'arcs', scatter_dim...  137 us
    all_to_all x2, blocking collectives, sent_to_all(): lax.all_to_all(jnp.broadcast_to(array[None], (count, *array.shape)), axis...  30.4 us
    dot_general x1, matrix products, contract_rows(): lax.dot_general(left, right, (((0,), (0,)), ((), ())), preferred_element_...  21.7 us
  transfers between devices with their start and end apart: 4, of which 4 were waited for; matrix products, arithmetic and copies ran while one was open for 1% of the time, Pallas kernels for 0%

commit v1 on v0

v1 whole, which is shorter than its diff:
```python
import jax
import jax.numpy as jnp
from jax import lax
from jax.sharding import Mesh
from jax.sharding import PartitionSpec as P

ARCS_DEV = 4
ARCS = ("x", "yh", "core")
TILES = ("z", "yl")
CHUNKS = 4
prior_rows = 4.0
f32, bf16 = jnp.float32, jnp.bfloat16


def of_everyone(array, axis):
    count = lax.axis_size(axis)
    sent = jnp.broadcast_to(array[None], (count, *array.shape))
    return lax.all_to_all(sent, axis, 0, 0, tiled=True).sum(axis=0)


def local(design, observations, solution, arc_ids, block_live):
    rows, cols = design.shape
    width = cols // CHUNKS
    core, yl = lax.axis_index("core"), lax.axis_index("yl")
    gathered = [
        lax.all_gather(design[:, j * width : (j + 1) * width], "z", axis=0)
        for j in range(CHUNKS)
    ]
    other = lax.ppermute(design, "yl", [(0, 1), (1, 0)])
    partial_value = jnp.dot(design.astype(f32), solution, precision=lax.Precision.HIGHEST)
    predicted = of_everyone(partial_value, TILES)
    residual = observations - predicted
    live_row = (
        jnp.broadcast_to(block_live[0][:, None], (block_live.shape[1], 128))
        .reshape(rows)
        .astype(f32)
    )
    arc_match = (arc_ids[0][None, :] == jnp.arange(ARCS_DEV, dtype=jnp.int32)[:, None]).astype(f32)
    squares = live_row * residual * residual
    arc_squares = jnp.sum(arc_match * squares[None, :], axis=1)
    arc_counts = jnp.sum(arc_match * live_row[None, :], axis=1)
    totals = of_everyone(jnp.stack([jnp.sum(arc_squares), jnp.sum(arc_counts)]), ARCS)
    variance_all = (totals[0] + 1.0) / (totals[1] + 1.0)
    arc_weight = variance_all / (
        (arc_squares + prior_rows * variance_all) / (arc_counts + prior_rows)
    )
    row_weight = live_row * jnp.sum(arc_match * arc_weight[:, None], axis=0)
    rhs_part = lax.dot_general(
        design.astype(f32),
        row_weight * residual,
        (((0,), (0,)), ((), ())),
        precision=lax.Precision.HIGHEST,
    )
    mine = jnp.where(core == yl, design, other)
    theirs = jnp.where(core == yl, other, design)
    weighted_mine = (row_weight[:, None] * mine).astype(bf16)
    weighted_theirs = (row_weight[:, None] * theirs).astype(bf16)

    def product(left, right):
        return lax.dot_general(left, right, (((1,), (0,)), ((), ())), preferred_element_type=f32)

    rank = lax.axis_index(("x", "yh"))
    done = []
    for j in range(CHUNKS):
        sent = product(gathered[j], weighted_theirs)
        kept = product(gathered[j], weighted_mine)
        pair = kept + lax.ppermute(sent, "core", [(0, 1), (1, 0)])
        got = lax.all_to_all(pair.astype(bf16), ("x", "yh"), 0, 0, tiled=True)
        done.append(jnp.sum(got.astype(f32), axis=0))
    block = jnp.concatenate(done, axis=0)
    swap = [(0, 0), (1, 2), (2, 1), (3, 3)]
    normal = lax.ppermute(block, ("core", "yl"), swap)
    rhs = of_everyone(rhs_part, ARCS)
    return normal, rhs


def solution(mesh):
    finer = Mesh(mesh.devices.reshape(4, 2, 2, 8, 2), ARCS + TILES)
    return jax.shard_map(
        local,
        mesh=finer,
        in_specs=(P(ARCS, TILES), P(ARCS), P(TILES), P(ARCS, None), P(ARCS, None)),
        out_specs=(P(ARCS, TILES), P(TILES)),
        check_vma=False,
    )
```

time: 502 us -> 302 us (0.60)
  waiting for transfers between devices: 417 us -> 158 us
  starting transfers between devices: 6.95 us -> 49.1 us
  other arithmetic: 2.98 us -> 21 us
  blocking collectives: 30.4 us -> 14.3 us
  matrix products: 23.8 us -> 35.6 us
    all_gather x2 -> x4, waiting for transfers between devices: 271 us -> 94.6 us  [local(): lax.all_gather(design[:, j * width:(j + 1) * width], 'z', axis=0)]
    reduce_scatter x1 -> x0, waiting for transfers between devices: 137 us -> none  [local(): lax.psum_scatter(contract_rows(design_all, weighted), 'arcs', scatter_dim...]
    all_to_all x1 -> x6, waiting for transfers between devices: 8.02 us -> 61.7 us  [the longest x4 31.1 us: local(): got = lax.all_to_all(pair.astype(bf16), ('x', 'yh'), 0, 0, tiled=True)]
    all_to_all x1 -> x6, starting transfers between devices: 6.84 us -> 39.1 us  [the longest x4 21.3 us: local(): got = lax.all_to_all(pair.astype(bf16), ('x', 'yh'), 0, 0, tiled=True)]
    all_to_all x2 -> x1, blocking collectives: 30.4 us -> 14.3 us  [of_everyone(): return lax.all_to_all(sent, axis, 0, 0, tiled=True).sum(axis=0)]
    convert_element_type x0 -> x5, other arithmetic: none -> 13.6 us  [the longest x4 11.1 us: local(): got = lax.all_to_all(pair.astype(bf16), ('x', 'yh'), 0, 0, tiled=True)]
    dot_general x3 -> x10, matrix products: 23.8 us -> 35.6 us  [the longest x8 33.5 us: product(): lax.dot_general(left, right, (((1,), (0,)), ((), ())), preferred_element_...]
    ppermute x0 -> x6, starting transfers between devices: none -> 9.81 us  [the longest x4 4.42 us: local(): pair = kept + lax.ppermute(sent, 'core', [(0, 1), (1, 0)])]
  transfers between devices with their start and end apart: 4 -> 16, of which waited for: 4 -> 8; matrix products, arithmetic and copies ran while one was open for 1% -> 19% of each run, Pallas kernels for 0% -> 0%
where the time goes in v1:
time: 302 us; the launch traced here: 301 us
  waiting for transfers between devices  158 us (52%)
  starting transfers between devices  49.1 us (16%)
  matrix products  35.6 us (12%)
  other arithmetic  21 us (7%)
  between operations  15.4 us (5%)
  blocking collectives  14.3 us (5%)
  local copies, waits for them, and re-layouts  7.22 us (2%)
    all_gather x4, waiting for transfers between devices, local(): lax.all_gather(design[:, j * width:(j + 1) * width], 'z', axis=0)  94.6 us
    dot_general x8, matrix products, product(): lax.dot_general(left, right, (((1,), (0,)), ((), ())), preferred_element_...  33.5 us
    all_to_all x4, waiting for transfers between devices, local(): got = lax.all_to_all(pair.astype(bf16), ('x', 'yh'), 0, 0, tiled=True)  31.1 us
    all_to_all x2, waiting for transfers between devices, of_everyone(): return lax.all_to_all(sent, axis, 0, 0, tiled=True).sum(axis=0)  30.5 us
    all_to_all x4, starting transfers between devices, local(): got = lax.all_to_all(pair.astype(bf16), ('x', 'yh'), 0, 0, tiled=True)  21.3 us
    all_to_all x2, starting transfers between devices, of_everyone(): return lax.all_to_all(sent, axis, 0, 0, tiled=True).sum(axis=0)  17.8 us
    all_to_all x1, blocking collectives, of_everyone(): return lax.all_to_all(sent, axis, 0, 0, tiled=True).sum(axis=0)  14.3 us
    convert_element_type x4, other arithmetic, local(): got = lax.all_to_all(pair.astype(bf16), ('x', 'yh'), 0, 0, tiled=True)  11.1 us
  transfers between devices with their start and end apart: 16, of which 8 were waited for; matrix products, arithmetic and copies ran while one was open for 19% of the time, Pallas kernels for 0%

profile of v1, /device:TPU:1, one launch (start us, length us, event | category | flops | bytes accessed | tf_op | source)
XLA Modules:
  0.0 300.8 jit_solution(1537398567657300323)
XLA Ops:
  7.2 0.0 copy-start
  7.2 0.0 all-gather.13.cloned.1.call-start
  7.2 2.7 fusion.7
  9.9 0.0 all-gather.13.cloned.1.call-update
  9.9 0.0 all-gather.11.cloned.1.call-start
  10.0 0.7 all-gather.11.cloned.1.call-update
  10.7 0.0 all-gather.9.cloned.1.call-start
  10.7 0.7 all-gather.9.cloned.1.call-update
  11.4 0.0 all-gather.15.cloned.1.call-start
  11.5 0.5 all-gather.15.cloned.1.call-update
  12.0 2.2 collective-permute-start
  14.2 1.3 convolution_reduce_fusion
  15.5 0.7 broadcast_in_dim.9
  16.2 8.3 %all-to-all-start = ((f32[16,1,1536]{2,1,0:T(1,128)}), f32[16,1,1536]{2,1,0:T(1,128)S(1)}, u32[]{:S(2)}, u32[]{:S(2)}) async-start(f32[16,1,1536]{2,1,0:T(1,128)} %broadcast_in_dim.9), calls=%async_computation | async-start | bytes 196608 | tf_op jit(solution)/shard_map/all_to_all | solution.py:18
  24.6 0.1 broadcast_bitcast_fusion
  24.7 23.5 %all-to-all-done = f32[16,1,1536]{2,1,0:T(1,128)S(1)} async-done(((f32[16,1,1536]{2,1,0:T(1,128)}), f32[16,1,1536]{2,1,0:T(1,128)S(1)}, u32[]{:S(2)}, u32[]{:S(2)}) %all-to-all-start) | async-done | bytes 98336 | tf_op jit(solution)/shard_map/all_to_all | solution.py:18
  48.2 0.1 reduce_sum.108
  48.3 0.1 multiply_multiply_fusion
  48.4 0.7 select_reduce_fusion.3
  49.0 1.4 pad_maximum_fusion.1
  50.4 0.6 broadcast_in_dim.10
  51.0 9.5 %all-to-all-start.1 = ((f32[16,1,2]{2,1,0:T(1,128)}), f32[16,1,2]{2,1,0:T(1,128)S(1)}, u32[]{:S(2)}, u32[]{:S(2)}) async-start(f32[16,1,2]{2,1,0:T(1,128)} %broadcast_in_dim.10), calls=%async_computation.1 | async-start | bytes 16384 | tf_op jit(solution)/shard_map/all_to_all | solution.py:18
  60.5 7.0 %all-to-all-done.1 = f32[16,1,2]{2,1,0:T(1,128)S(1)} async-done(((f32[16,1,2]{2,1,0:T(1,128)}), f32[16,1,2]{2,1,0:T(1,128)S(1)}, u32[]{:S(2)}, u32[]{:S(2)}) %all-to-all-start.1) | async-done | bytes 160 | tf_op jit(solution)/shard_map/all_to_all | solution.py:18
  67.6 0.6 fusion.8
  69.6 0.1 select_reduce_fusion.4
  69.7 0.1 fusion.6
  69.7 0.0 collective-permute-done
  69.8 2.5 fusion.4
  72.2 5.6 %convolution_bitcast_fusion.1 = f32[8,128,512]{1,2,0:T(8,128)} fusion(bf16[1536,512,1]{1,0,2:T(8,128)(2,1)} %get-tuple-element.19, bf16[8,1536,128]{2,1,0:T(8,128)(2,1)} %bitcast.78), kind=kOutput, calls=%fused_computation.15 | convolution fusion | flops 1610612736 | bytes 6815744 | tf_op jit(solution)/shard_map/dot_general | solution.py:60
  77.8 0.7 collective-permute-start.3
  78.5 27.1 %all-gather.11.cloned.1.call-done = bf16[12288,128]{1,0:T(8,128)(2,1)} async-done(((bf16[1536,128]{1,0:T(8,128)(2,1)}), bf16[12288,128]{1,0:T(8,128)(2,1)}) %all-gather.11.cloned.1.call-update) | async-done | bytes 3145744 | tf_op jit(solution)/shard_map/all_gather | solution.py:26
  105.7 5.1 %convolution_bitcast_fusion.2 = f32[8,128,512]{1,2,0:T(8,128)} fusion(bf16[1536,512,1]{1,0,2:T(8,128)(2,1)S(1)} %copy-done.4, bf16[8,1536,128]{2,1,0:T(8,128)(2,1)} %bitcast.76), kind=kOutput, calls=%fused_computation.16 | convolution fusion | flops 1610612736 | bytes 6815744 | tf_op jit(solution)/shard_map/dot_general | solution.py:60
  110.7 1.2 collective-permute-start.2
  111.9 39.7 %all-gather.9.cloned.1.call-done = bf16[12288,128]{1,0:T(8,128)(2,1)} async-done(((bf16[1536,128]{1,0:T(8,128)(2,1)}), bf16[12288,128]{1,0:T(8,128)(2,1)}) %all-gather.9.cloned.1.call-update) | async-done | bytes 3145744 | tf_op jit(solution)/shard_map/all_gather | solution.py:26
  151.7 5.2 %convolution_bitcast_fusion.3 = f32[8,128,512]{1,2,0:T(8,128)} fusion(bf16[1536,512,1]{1,0,2:T(8,128)(2,1)S(1)} %copy-done.4, bf16[8,1536,128]{2,1,0:T(8,128)(2,1)} %bitcast.74), kind=kOutput, calls=%fused_computation.17 | convolution fusion | flops 1610612736 | bytes 6815744 | tf_op jit(solution)/shard_map/dot_general | solution.py:60
  156.9 1.2 collective-permute-start.1
  158.1 1.8 fusion.11
  160.0 2.8 fusion.1
  162.7 6.4 %all-to-all-start.4 = ((bf16[8,128,512]{1,2,0:T(8,128)(2,1)}), bf16[8,128,512]{1,2,0:T(8,128)(2,1)S(1)}, u32[]{:S(2)}, u32[]{:S(2)}) async-start(bf16[8,128,512]{1,2,0:T(8,128)(2,1)} %fusion.1), calls=%async_computation.4 | async-start | bytes 2097152 | tf_op jit(solution)/shard_map/all_to_all | solution.py:68
  169.2 27.8 %all-gather.15.cloned.1.call-done = bf16[12288,128]{1,0:T(8,128)(2,1)} async-done(((bf16[1536,128]{1,0:T(8,128)(2,1)}), bf16[12288,128]{1,0:T(8,128)(2,1)}) %all-gather.15.cloned.1.call-update) | async-done | bytes 3145744 | tf_op jit(solution)/shard_map/all_gather | solution.py:26
  197.0 5.6 %convolution_bitcast_fusion = f32[8,128,512]{1,2,0:T(8,128)} fusion(bf16[1536,512,1]{1,0,2:T(8,128)(2,1)} %get-tuple-element.19, bf16[8,1536,128]{2,1,0:T(8,128)(2,1)} %bitcast.72), kind=kOutput, calls=%fused_computation.14 | convolution fusion | flops 1610612736 | bytes 6815744 | tf_op jit(solution)/shard_map/dot_general | solution.py:60
  202.6 1.2 collective-permute-start.4
  203.8 1.8 fusion.10
  205.7 2.8 fusion.2
  208.5 6.4 %all-to-all-start.3 = ((bf16[8,128,512]{1,2,0:T(8,128)(2,1)}), bf16[8,128,512]{1,2,0:T(8,128)(2,1)}, u32[]{:S(2)}, u32[]{:S(2)}) async-start(bf16[8,128,512]{1,2,0:T(8,128)(2,1)} %fusion.2), calls=%async_computation.3 | async-start | bytes 2097152 | tf_op jit(solution)/shard_map/all_to_all | solution.py:68
  214.9 4.2 %fusion.9 = f32[512,8,128]{2,0,1:T(8,128)S(1)} fusion(bf16[1536,512,1]{1,0,2:T(8,128)(2,1)} %get-tuple-element.18, bf16[8,1536,128]{2,1,0:T(8,128)(2,1)} %bitcast.75), kind=kOutput, calls=%fused_computation.37 | convolution fusion | flops 1610612736 | bytes 6815744 | tf_op jit(solution)/shard_map/dot_general | solution.py:60
  219.1 2.8 fusion.3
  221.9 9.6 %all-to-all-done.3 = bf16[8,128,512]{1,2,0:T(8,128)(2,1)} async-done(((bf16[8,128,512]{1,2,0:T(8,128)(2,1)}), bf16[8,128,512]{1,2,0:T(8,128)(2,1)}, u32[]{:S(2)}, u32[]{:S(2)}) %all-to-all-start.3) | async-done | bytes 1048608 | tf_op jit(solution)/shard_map/all_to_all | solution.py:68
  231.5 4.2 %all-to-all-start.2 = ((bf16[8,128,512]{1,2,0:T(8,128)(2,1)}), bf16[8,128,512]{1,2,0:T(8,128)(2,1)}, u32[]{:S(2)}, u32[]{:S(2)}) async-start(bf16[8,128,512]{1,2,0:T(8,128)(2,1)} %fusion.3), calls=%async_computation.2 | async-start | bytes 2097152 | tf_op jit(solution)/shard_map/all_to_all | solution.py:68
  235.7 4.2 %fusion.12 = f32[512,8,128]{2,0,1:T(8,128)S(1)} fusion(bf16[1536,512,1]{1,0,2:T(8,128)(2,1)} %get-tuple-element.18, bf16[8,1536,128]{2,1,0:T(8,128)(2,1)} %bitcast.73), kind=kOutput, calls=%fused_computation.40 | convolution fusion | flops 1610612736 | bytes 6815744 | tf_op jit(solution)/shard_map/dot_general | solution.py:60
  239.9 2.8 fusion
  242.7 8.7 %all-to-all-done.2 = bf16[8,128,512]{1,2,0:T(8,128)(2,1)} async-done(((bf16[8,128,512]{1,2,0:T(8,128)(2,1)}), bf16[8,128,512]{1,2,0:T(8,128)(2,1)}, u32[]{:S(2)}, u32[]{:S(2)}) %all-to-all-start.2) | async-done | bytes 1048608 | tf_op jit(solution)/shard_map/all_to_all | solution.py:68
  251.4 4.2 %all-to-all-start.5 = ((bf16[8,128,512]{1,2,0:T(8,128)(2,1)}), bf16[8,128,512]{1,2,0:T(8,128)(2,1)}, u32[]{:S(2)}, u32[]{:S(2)}) async-start(bf16[8,128,512]{1,2,0:T(8,128)(2,1)} %fusion), calls=%async_computation.5 | async-start | bytes 2097152 | tf_op jit(solution)/shard_map/all_to_all | solution.py:68
  255.7 0.1 convert_reduce_fusion.1
  255.8 1.4 convert_reduce_fusion.2
  257.2 1.4 convert_reduce_fusion.3
  258.6 12.7 %all-to-all-done.5 = bf16[8,128,512]{1,2,0:T(8,128)(2,1)} async-done(((bf16[8,128,512]{1,2,0:T(8,128)(2,1)}), bf16[8,128,512]{1,2,0:T(8,128)(2,1)}, u32[]{:S(2)}, u32[]{:S(2)}) %all-to-all-start.5) | async-done | bytes 1048608 | tf_op jit(solution)/shard_map/all_to_all | solution.py:68
  271.4 1.4 convert_reduce_fusion
  272.8 0.1 pad_maximum_fusion
  272.8 3.2 %collective-permute-start.5 = (f32[512,512]{0,1:T(8,128)S(1)}, f32[512,512]{0,1:T(8,128)}, u32[]{:S(2)}, u32[]{:S(2)}) collective-permute-start(f32[512,512]{0,1:T(8,128)S(1)} %pad_maximum_fusion), channel_id=1, source_target_pairs={{0,0},{1,16},{16,1},{17,17},{2,2},{3,18},{18,3},{19,19},{4,4},{5,2... | collective-permute-start | bytes 3145736 | tf_op jit(solution)/shard_map/ppermute | solution.py:72
  276.0 0.7 fusion.13
  276.8 14.3 %all_to_all.38 = f32[16,1,512]{2,1,0:T(1,128)S(1)} all-to-all(f32[16,1,512]{2,1,0:T(1,128)S(1)} %broadcast_in_dim.11), channel_id=1, replica_groups=mesh['x'=4,'yh'=2,'core'=2,'z'=8,'yl'=2] {'x','yh','core'}, dimensions={0} | all-to-all | bytes 65536 | tf_op jit(solution)/shard_map/all_to_all | solution.py:18
  291.1 0.6 reduce_sum.119
  291.8 2.5 copy.44
  (32 shorter events, 0.2 us)
Async XLA Ops:
  7.2 7.0 %copy-start = (f32[512]{0:T(512)S(1)}, f32[512]{0:T(512)}, u32[]{:S(2)}) copy-start(f32[512]{0:T(512)} %param.7) | copy-start | bytes 6148
  7.2 4.8 %copy-start.1 = (bf16[1536,512]{1,0:T(8,128)(2,1)S(1)}, bf16[1536,512]{1,0:T(8,128)(2,1)}, u32[]{:S(2)}) copy-start(bf16[1536,512]{1,0:T(8,128)(2,1)} %param.5) | copy-start | bytes 4718596
  7.2 65.0 %all-gather.13.cloned.1.call-start = ((), (), s32[]{:S(2)}) async-start(), calls=%async_computation.9 | async-start | bytes 3538944 | tf_op jit(solution)/shard_map/all_gather | solution.py:26
  9.9 14.7 %copy-start.6 = (s32[1,1536]{1,0:T(1,128)S(1)}, s32[1,1536]{1,0:T(1,128)}, u32[]{:S(2)}) copy-start(s32[1,1536]{1,0:T(1,128)} %param.8) | copy-start | bytes 18436
  9.9 14.7 %copy-start.9 = (s32[1,12]{1,0:T(1,128)S(1)}, s32[1,12]{1,0:T(1,128)}, u32[]{:S(2)}) copy-start(s32[1,12]{1,0:T(1,128)} %param.9) | copy-start | bytes 148
  9.9 38.4 %copy-start.5 = (f32[1536]{0:T(1024)S(1)}, f32[1536]{0:T(1024)}, u32[]{:S(2)}) copy-start(f32[1536]{0:T(1024)} %param.6) | copy-start | bytes 18436
  9.9 95.7 %all-gather.11.cloned.1.call-start = ((), (), s32[]{:S(2)}) async-start(), calls=%async_computation.8 | async-start | bytes 3538944 | tf_op jit(solution)/shard_map/all_gather | solution.py:26
  10.7 141.0 %all-gather.9.cloned.1.call-start = ((), (), s32[]{:S(2)}) async-start(), calls=%async_computation.7 | async-start | bytes 3538944 | tf_op jit(solution)/shard_map/all_gather | solution.py:26
  11.4 185.5 %all-gather.15.cloned.1.call-start = ((), (), s32[]{:S(2)}) async-start(), calls=%async_computation.10 | async-start | bytes 3538944 | tf_op jit(solution)/shard_map/all_gather | solution.py:26
  12.0 57.8 %collective-permute-start = (bf16[1536,512]{1,0:T(8,128)(2,1)S(1)}, bf16[1536,512]{1,0:T(8,128)(2,1)S(1)}, u32[]{:S(2)}, u32[]{:S(2)}) collective-permute-start(bf16[1536,512]{1,0:T(8,128)(2,1)S(1)} %copy-done.1), channel_id=1, source_target_pairs={{0,1},{1,0},{2,3},{3,2},{4,5},{5,4},{6,7},{7,6},{8,9},{9,8},{10,11... | collective-permute-start | bytes 4718600 | tf_op jit(solution)/shard_map/ppermute | solution.py:29
  16.2 32.0 %all-to-all-start = ((f32[16,1,1536]{2,1,0:T(1,128)}), f32[16,1,1536]{2,1,0:T(1,128)S(1)}, u32[]{:S(2)}, u32[]{:S(2)}) async-start(f32[16,1,1536]{2,1,0:T(1,128)} %broadcast_in_dim.9), calls=%async_computation | async-start | bytes 196608 | tf_op jit(solution)/shard_map/all_to_all | solution.py:18
  51.0 16.5 %all-to-all-start.1 = ((f32[16,1,2]{2,1,0:T(1,128)}), f32[16,1,2]{2,1,0:T(1,128)S(1)}, u32[]{:S(2)}, u32[]{:S(2)}) async-start(f32[16,1,2]{2,1,0:T(1,128)} %broadcast_in_dim.10), calls=%async_computation.1 | async-start | bytes 16384 | tf_op jit(solution)/shard_map/all_to_all | solution.py:18
  72.2 33.4 %copy-start.4 = (bf16[1536,512,1]{1,0,2:T(8,128)(2,1)S(1)}, bf16[1536,512,1]{1,0,2:T(8,128)(2,1)}, u32[]{:S(2)}) copy-start(bf16[1536,512,1]{1,0,2:T(8,128)(2,1)} %get-tuple-element.19) | copy-start | bytes 4718596
  77.8 82.1 %collective-permute-start.3 = (f32[8,128,512]{1,2,0:T(8,128)}, f32[8,128,512]{1,2,0:T(8,128)}, u32[]{:S(2)}, u32[]{:S(2)}) collective-permute-start(f32[8,128,512]{1,2,0:T(8,128)} %convolution_bitcast_fusion.1), channel_id=1, source_target_pairs={{0,16},{16,0},{1,17},{17,1},{2,18},{18,2},{3,19},{19,3},{4,20},{20... | collective-permute-start | bytes 6291464 | tf_op jit(solution)/shard_map/ppermute | solution.py:67
  110.7 95.0 %collective-permute-start.2 = (f32[8,128,512]{1,2,0:T(8,128)}, f32[8,128,512]{1,2,0:T(8,128)}, u32[]{:S(2)}, u32[]{:S(2)}) collective-permute-start(f32[8,128,512]{1,2,0:T(8,128)} %convolution_bitcast_fusion.2), channel_id=1, source_target_pairs={{0,16},{16,0},{1,17},{17,1},{2,18},{18,2},{3,19},{19,3},{4,20},{20... | collective-permute-start | bytes 6291464 | tf_op jit(solution)/shard_map/ppermute | solution.py:67
  151.7 6.5 %copy-start.2 = (bf16[1536,512,1]{1,0,2:T(8,128)(2,1)S(1)}, bf16[1536,512,1]{1,0,2:T(8,128)(2,1)}, u32[]{:S(2)}) copy-start(bf16[1536,512,1]{1,0,2:T(8,128)(2,1)} %get-tuple-element.18) | copy-start | bytes 4718596
  151.7 6.5 %copy-start.8 = (bf16[12288,128]{1,0:T(8,128)(2,1)S(1)}, bf16[12288,128]{1,0:T(8,128)(2,1)}, u32[]{:S(2)}) copy-start(bf16[12288,128]{1,0:T(8,128)(2,1)} %all-gather.13.cloned.1.call-done) | copy-start | bytes 9437188
  156.9 62.2 %collective-permute-start.1 = (f32[8,128,512]{1,2,0:T(8,128)}, f32[8,128,512]{1,2,0:T(8,128)}, u32[]{:S(2)}, u32[]{:S(2)}) collective-permute-start(f32[8,128,512]{1,2,0:T(8,128)} %convolution_bitcast_fusion.3), channel_id=1, source_target_pairs={{0,16},{16,0},{1,17},{17,1},{2,18},{18,2},{3,19},{19,3},{4,20},{20... | collective-permute-start | bytes 6291464 | tf_op jit(solution)/shard_map/ppermute | solution.py:67
  162.7 45.7 %all-to-all-start.4 = ((bf16[8,128,512]{1,2,0:T(8,128)(2,1)}), bf16[8,128,512]{1,2,0:T(8,128)(2,1)S(1)}, u32[]{:S(2)}, u32[]{:S(2)}) async-start(bf16[8,128,512]{1,2,0:T(8,128)(2,1)} %fusion.1), calls=%async_computation.4 | async-start | bytes 2097152 | tf_op jit(solution)/shard_map/all_to_all | solution.py:68
  196.9 6.9 %copy-start.3 = (bf16[1536,512,1]{1,0,2:T(8,128)(2,1)S(1)}, bf16[1536,512,1]{1,0,2:T(8,128)(2,1)}, u32[]{:S(2)}) copy-start(bf16[1536,512,1]{1,0,2:T(8,128)(2,1)} %get-tuple-element.18) | copy-start | bytes 4718596
  197.0 6.9 %copy-start.7 = (bf16[12288,128]{1,0:T(8,128)(2,1)S(1)}, bf16[12288,128]{1,0:T(8,128)(2,1)}, u32[]{:S(2)}) copy-start(bf16[12288,128]{1,0:T(8,128)(2,1)} %all-gather.11.cloned.1.call-done) | copy-start | bytes 9437188
  202.6 37.3 %collective-permute-start.4 = (f32[8,128,512]{1,2,0:T(8,128)}, f32[8,128,512]{1,2,0:T(8,128)}, u32[]{:S(2)}, u32[]{:S(2)}) collective-permute-start(f32[8,128,512]{1,2,0:T(8,128)} %convolution_bitcast_fusion), channel_id=1, source_target_pairs={{0,16},{16,0},{1,17},{17,1},{2,18},{18,2},{3,19},{19,3},{4,20},{20... | collective-permute-start | bytes 6291464 | tf_op jit(solution)/shard_map/ppermute | solution.py:67
  208.5 23.0 %all-to-all-start.3 = ((bf16[8,128,512]{1,2,0:T(8,128)(2,1)}), bf16[8,128,512]{1,2,0:T(8,128)(2,1)}, u32[]{:S(2)}, u32[]{:S(2)}) async-start(bf16[8,128,512]{1,2,0:T(8,128)(2,1)} %fusion.2), calls=%async_computation.3 | async-start | bytes 2097152 | tf_op jit(solution)/shard_map/all_to_all | solution.py:68
  231.5 19.9 %all-to-all-start.2 = ((bf16[8,128,512]{1,2,0:T(8,128)(2,1)}), bf16[8,128,512]{1,2,0:T(8,128)(2,1)}, u32[]{:S(2)}, u32[]{:S(2)}) async-start(bf16[8,128,512]{1,2,0:T(8,128)(2,1)} %fusion.3), calls=%async_computation.2 | async-start | bytes 2097152 | tf_op jit(solution)/shard_map/all_to_all | solution.py:68
  251.4 19.9 %all-to-all-start.5 = ((bf16[8,128,512]{1,2,0:T(8,128)(2,1)}), bf16[8,128,512]{1,2,0:T(8,128)(2,1)}, u32[]{:S(2)}, u32[]{:S(2)}) async-start(bf16[8,128,512]{1,2,0:T(8,128)(2,1)} %fusion), calls=%async_computation.5 | async-start | bytes 2097152 | tf_op jit(solution)/shard_map/all_to_all | solution.py:68
  272.8 18.9 %collective-permute-start.5 = (f32[512,512]{0,1:T(8,128)S(1)}, f32[512,512]{0,1:T(8,128)}, u32[]{:S(2)}, u32[]{:S(2)}) collective-permute-start(f32[512,512]{0,1:T(8,128)S(1)} %pad_maximum_fusion), channel_id=1, source_target_pairs={{0,0},{1,16},{16,1},{17,17},{2,2},{3,18},{18,3},{19,19},{4,4},{5,2... | collective-permute-start | bytes 3145736 | tf_op jit(solution)/shard_map/ppermute | solution.py:72
Sparse Core Ops, SparseCore 0:
  10.0 49.9 all-gather.12
  61.8 43.7 all-gather.10
  108.0 43.5 all-gather.8
  153.3 43.5 all-gather.14

commit v2 on v1

--- a/solution.py
+++ b/solution.py
@@ -7,9 +7,14 @@
 ARCS_DEV = 4
 ARCS = ("x", "yh", "core")
 TILES = ("z", "yl")
-CHUNKS = 4
+WIDTHS = (256, 128, 128)
+PAIR = [(0, 1), (1, 0)]
 prior_rows = 4.0
 f32, bf16 = jnp.float32, jnp.bfloat16
+
+
+def after(array, *first):
+    return lax.optimization_barrier((array, *first))[0]
 
 
 def of_everyone(array, axis):
@@ -19,16 +24,16 @@
 
 
 def local(design, observations, solution, arc_ids, block_live):
-    rows, cols = design.shape
-    width = cols // CHUNKS
+    rows, _ = design.shape
     core, yl = lax.axis_index("core"), lax.axis_index("yl")
-    gathered = [
-        lax.all_gather(design[:, j * width : (j + 1) * width], "z", axis=0)
-        for j in range(CHUNKS)
-    ]
-    other = lax.ppermute(design, "yl", [(0, 1), (1, 0)])
+    gathered, begin = [], 0
+    for width in WIDTHS:
+        gathered.append(lax.all_gather(design[:, begin : begin + width], "z", axis=0))
+        begin += width
     partial_value = jnp.dot(design.astype(f32), solution, precision=lax.Precision.HIGHEST)
-    predicted = of_everyone(partial_value, TILES)
+    from_pair = lax.ppermute(partial_value, "yl", PAIR)
+    other = lax.ppermute(after(design, from_pair), "yl", PAIR)
+    predicted = of_everyone(partial_value + from_pair, "z")
     residual = observations - predicted
     live_row = (
         jnp.broadcast_to(block_live[0][:, None], (block_live.shape[1], 128))
@@ -51,27 +56,25 @@
         (((0,), (0,)), ((), ())),
         precision=lax.Precision.HIGHEST,
     )
-    mine = jnp.where(core == yl, design, other)
-    theirs = jnp.where(core == yl, other, design)
-    weighted_mine = (row_weight[:, None] * mine).astype(bf16)
-    weighted_theirs = (row_weight[:, None] * theirs).astype(bf16)
+    rhs_pair = rhs_part + lax.ppermute(rhs_part, "core", PAIR)
+    rhs = of_everyone(rhs_pair, ("x", "yh"))
+    weighted_own = (row_weight[:, None] * design).astype(bf16)
+    weighted_other = (row_weight[:, None] * other).astype(bf16)
+    mine = jnp.where(core == yl, weighted_own, weighted_other)
+    theirs = jnp.where(core == yl, weighted_other, weighted_own)
 
     def product(left, right):
         return lax.dot_general(left, right, (((1,), (0,)), ((), ())), preferred_element_type=f32)
 
-    rank = lax.axis_index(("x", "yh"))
-    done = []
-    for j in range(CHUNKS):
-        sent = product(gathered[j], weighted_theirs)
-        kept = product(gathered[j], weighted_mine)
-        pair = kept + lax.ppermute(sent, "core", [(0, 1), (1, 0)])
-        got = lax.all_to_all(pair.astype(bf16), ("x", "yh"), 0, 0, tiled=True)
-        done.append(jnp.sum(got.astype(f32), axis=0))
-    block = jnp.concatenate(done, axis=0)
-    swap = [(0, 0), (1, 2), (2, 1), (3, 3)]
-    normal = lax.ppermute(block, ("core", "yl"), swap)
-    rhs = of_everyone(rhs_part, ARCS)
-    return normal, rhs
+    done, swap = [], [(0, 0), (1, 2), (2, 1), (3, 3)]
+    for j, left in enumerate(gathered):
+        sent = product(left, theirs if j else after(theirs, rhs))
+        from_core = lax.ppermute(sent, "core", PAIR)
+        pair = (product(left, mine) + from_core).astype(bf16)
+        got = lax.all_to_all(pair, ("x", "yh"), 0, 0, tiled=True)
+        block = jnp.sum(got.astype(f32), axis=0)
+        done.append(lax.ppermute(block, ("core", "yl"), swap))
+    return jnp.concatenate(done, axis=0), rhs
 
 
 def solution(mesh):

time: 302 us -> 284 us (0.940)
  waiting for transfers between devices: 158 us -> 140 us
  blocking collectives: 14.3 us -> 29.4 us
  other arithmetic: 21 us -> 12.1 us
  starting transfers between devices: 49.1 us -> 43.6 us
    all_to_all x2, waiting for transfers between devices: 30.5 us -> 12.3 us  [of_everyone(): return lax.all_to_all(sent, axis, 0, 0, tiled=True).sum(axis=0)]
    all_to_all x1, blocking collectives: 14.3 us -> 29.4 us  [of_everyone(): return lax.all_to_all(sent, axis, 0, 0, tiled=True).sum(axis=0)]
    all_gather x4 -> x3, waiting for transfers between devices: 94.6 us -> 81.9 us  [local(): gathered.append(lax.all_gather(design[:, begin:begin + width], 'z', axis=0))]
    convert_element_type x5 -> x2, other arithmetic: 13.6 us -> 3.95 us  [local(): pair = (product(left, mine) + from_core).astype(bf16)]
    all_to_all x4 -> x3, waiting for transfers between devices: 31.1 us -> 40.1 us  [local(): got = lax.all_to_all(pair, ('x', 'yh'), 0, 0, tiled=True)]
    all_to_all x4 -> x3, starting transfers between devices: 21.3 us -> 14.4 us  [local(): got = lax.all_to_all(pair, ('x', 'yh'), 0, 0, tiled=True)]
    ppermute x6 -> x9, starting transfers between devices: 9.81 us -> 16.6 us  [the longest x3 9.19 us: local(): done.append(lax.ppermute(block, ('core', 'yl'), swap))]
    ppermute x6 -> x9, waiting for transfers between devices: 0.02 us -> 6 us  [the longest x3 4.17 us: local(): done.append(lax.ppermute(block, ('core', 'yl'), swap))]
  transfers between devices with their start and end apart: 16 -> 17, of which waited for: 8 -> 12; matrix products, arithmetic and copies ran while one was open for 19% -> 18% of each run, Pallas kernels for 0% -> 0%
where the time goes in v2:
time: 284 us; the launch traced here: 283 us
  waiting for transfers between devices  140 us (49%)
  starting transfers between devices  43.6 us (15%)
  matrix products  35.8 us (13%)
  blocking collectives  29.4 us (10%)
  between operations  15.3 us (5%)
  other arithmetic  12.1 us (4%)
  local copies, waits for them, and re-layouts  6.42 us (2%)
    all_gather x3, waiting for transfers between devices, local(): gathered.append(lax.all_gather(design[:, begin:begin + width], 'z', axis=0))  81.9 us
    all_to_all x3, waiting for transfers between devices, local(): got = lax.all_to_all(pair, ('x', 'yh'), 0, 0, tiled=True)  40.1 us
    dot_general x6, matrix products, product(): lax.dot_general(left, right, (((1,), (0,)), ((), ())), preferred_element_...  33.7 us
    all_to_all x1, blocking collectives, of_everyone(): return lax.all_to_all(sent, axis, 0, 0, tiled=True).sum(axis=0)  29.4 us
    all_to_all x3, starting transfers between devices, local(): got = lax.all_to_all(pair, ('x', 'yh'), 0, 0, tiled=True)  14.4 us
    all_to_all x2, starting transfers between devices, of_everyone(): return lax.all_to_all(sent, axis, 0, 0, tiled=True).sum(axis=0)  12.5 us
    all_to_all x2, waiting for transfers between devices, of_everyone(): return lax.all_to_all(sent, axis, 0, 0, tiled=True).sum(axis=0)  12.3 us
    ppermute x3, starting transfers between devices, local(): done.append(lax.ppermute(block, ('core', 'yl'), swap))  9.19 us
  transfers between devices with their start and end apart: 17, of which 12 were waited for; matrix products, arithmetic and copies ran while one was open for 18% of the time, Pallas kernels for 0%

profile of v2, /device:TPU:1, one launch (start us, length us, event | category | flops | bytes accessed | tf_op | source)
XLA Modules:
  0.0 282.9 jit_solution(8241127200260774900)
XLA Ops:
  7.2 0.0 copy-start
  7.2 0.0 all-gather.7.cloned.1.call-start
  7.2 2.2 slice.17
  9.4 0.0 all-gather.7.cloned.1.call-update
  9.4 0.0 copy-start.6
  9.5 0.0 copy-start.5
  9.5 0.0 all-gather.11.cloned.1.call-start
  9.5 1.0 fusion.12
  10.5 0.0 all-gather.11.cloned.1.call-update
  10.5 0.0 all-gather.9.cloned.1.call-start
  10.6 1.3 convolution_reduce_fusion
  11.9 2.2 collective-permute-start
  14.1 0.0 all-gather.9.cloned.1.call-update
  14.2 1.0 collective-permute-done
  15.2 0.6 broadcast_in_dim.9
  15.8 8.3 %all-to-all-start = ((f32[8,1,1536]{2,1,0:T(1,128)}), f32[8,1,1536]{2,1,0:T(1,128)S(1)}, u32[]{:S(2)}, u32[]{:S(2)}) async-start(f32[8,1,1536]{2,1,0:T(1,128)} %broadcast_in_dim.9), calls=%async_computation | async-start | bytes 98304 | tf_op jit(solution)/shard_map/all_to_all | solution.py:23
  24.2 1.3 collective-permute-start.1
  25.5 0.1 broadcast_bitcast_fusion
  25.6 5.8 %all-to-all-done = f32[8,1,1536]{2,1,0:T(1,128)S(1)} async-done(((f32[8,1,1536]{2,1,0:T(1,128)}), f32[8,1,1536]{2,1,0:T(1,128)S(1)}, u32[]{:S(2)}, u32[]{:S(2)}) %all-to-all-start) | async-done | bytes 49184 | tf_op jit(solution)/shard_map/all_to_all | solution.py:23
  31.4 0.1 multiply_multiply_fusion
  31.4 0.7 select_reduce_fusion.3
  32.1 1.3 pad_maximum_fusion.1
  33.5 29.4 %all_to_all.33 = f32[16,1,2]{2,1,0:T(1,128)S(1)} all-to-all(f32[16,1,2]{2,1,0:T(1,128)S(1)} %broadcast_in_dim.10), channel_id=1, replica_groups=mesh['x'=4,'yh'=2,'core'=2,'z'=8,'yl'=2] {'x','yh','core'}, dimensions={0} | all-to-all | bytes 256 | tf_op jit(solution)/shard_map/all_to_all | solution.py:23
  62.9 0.6 fusion.13
  64.8 0.1 select_reduce_fusion.4
  64.9 0.1 fusion.11
  65.0 0.7 fusion.14
  65.7 0.6 collective-permute-start.2
  66.3 0.8 collective-permute-done.2
  67.2 0.6 broadcast_in_dim.11
  67.8 4.1 %all-to-all-start.2 = ((f32[8,1,512]{2,1,0:T(1,128)}), f32[8,1,512]{2,1,0:T(1,128)S(1)}, u32[]{:S(2)}, u32[]{:S(2)}) async-start(f32[8,1,512]{2,1,0:T(1,128)} %broadcast_in_dim.11), calls=%async_computation.2 | async-start | bytes 32768 | tf_op jit(solution)/shard_map/all_to_all | solution.py:23
  71.9 6.5 %all-to-all-done.2 = f32[8,1,512]{2,1,0:T(1,128)S(1)} async-done(((f32[8,1,512]{2,1,0:T(1,128)}), f32[8,1,512]{2,1,0:T(1,128)S(1)}, u32[]{:S(2)}, u32[]{:S(2)}) %all-to-all-start.2) | async-done | bytes 16416 | tf_op jit(solution)/shard_map/all_to_all | solution.py:23
  78.5 0.6 reduce_sum.106
  79.1 2.5 broadcast_select_fusion.1
  81.5 7.7 %all-gather.7.cloned.1.call-done = bf16[12288,256]{1,0:T(8,128)(2,1)} async-done(((bf16[1536,256]{1,0:T(8,128)(2,1)}), bf16[12288,256]{1,0:T(8,128)(2,1)}) %all-gather.7.cloned.1.call-update) | async-done | bytes 6291472 | tf_op jit(solution)/shard_map/all_gather | solution.py:31
  89.3 8.9 %convolution_bitcast_fusion = f32[8,256,512]{1,2,0:T(8,128)} fusion(bf16[8,1536,256]{2,1,0:T(8,128)(2,1)} %bitcast.64, bf16[1536,512]{1,0:T(8,128)(2,1)} %get-tuple-element.5), kind=kOutput, calls=%fused_computation.5 | convolution fusion | flops 3221225472 | bytes 12058624 | tf_op jit(solution)/shard_map/dot_general | solution.py:67
  98.2 0.8 collective-permute-start.3
  98.9 35.0 %all-gather.11.cloned.1.call-done = bf16[12288,128]{1,0:T(8,128)(2,1)} async-done(((bf16[1536,128]{1,0:T(8,128)(2,1)}), bf16[12288,128]{1,0:T(8,128)(2,1)}) %all-gather.11.cloned.1.call-update) | async-done | bytes 3145744 | tf_op jit(solution)/shard_map/all_gather | solution.py:31
  134.0 5.1 %convolution_bitcast_fusion.1 = f32[8,128,512]{1,2,0:T(8,128)} fusion(bf16[8,1536,128]{2,1,0:T(8,128)(2,1)} %bitcast.68, bf16[1536,512]{1,0:T(8,128)(2,1)S(1)} %copy-done.4), kind=kOutput, calls=%fused_computation.12 | convolution fusion | flops 1610612736 | bytes 6815744 | tf_op jit(solution)/shard_map/dot_general | solution.py:67
  139.1 1.2 collective-permute-start.7
  140.3 39.1 %all-gather.9.cloned.1.call-done = bf16[12288,128]{1,0:T(8,128)(2,1)} async-done(((bf16[1536,128]{1,0:T(8,128)(2,1)}), bf16[12288,128]{1,0:T(8,128)(2,1)}) %all-gather.9.cloned.1.call-update) | async-done | bytes 3145744 | tf_op jit(solution)/shard_map/all_gather | solution.py:31
  179.4 5.6 %convolution_bitcast_fusion.2 = f32[8,128,512]{1,2,0:T(8,128)} fusion(bf16[8,1536,128]{2,1,0:T(8,128)(2,1)} %bitcast.66, bf16[1536,512]{1,0:T(8,128)(2,1)} %get-tuple-element.5), kind=kOutput, calls=%fused_computation.13 | convolution fusion | flops 1610612736 | bytes 6815744 | tf_op jit(solution)/shard_map/dot_general | solution.py:67
  185.1 1.2 collective-permute-start.5
  186.3 1.8 fusion.6
  188.2 1.2 fusion.1
  189.3 6.6 %all-to-all-start.5 = ((bf16[8,128,512]{1,2,0:T(8,128)(2,1)}), bf16[8,128,512]{1,2,0:T(8,128)(2,1)S(1)}, u32[]{:S(2)}, u32[]{:S(2)}) async-start(bf16[8,128,512]{1,2,0:T(8,128)(2,1)} %fusion.1), calls=%async_computation.5 | async-start | bytes 2097152 | tf_op jit(solution)/shard_map/all_to_all | solution.py:74
  195.9 8.1 %fusion = bf16[8,256,512]{1,2,0:T(8,128)(2,1)} fusion(f32[8,256,512]{1,2,0:T(8,128)} %collective-permute-done.3, bf16[8,1536,256]{2,1,0:T(8,128)(2,1)} %bitcast.65, bf16[1536,512]{1,0:T(8,128)(2,1)S(1)} %copy-done.3), kind=kOutput, calls=%fused_computation.1 | convolution fusion | flops 3223322624 | bytes 14155776 | tf_op jit(solution)/shard_map/dot_general | solution.py:67
  204.0 8.4 %all-to-all-done.5 = bf16[8,128,512]{1,2,0:T(8,128)(2,1)S(1)} async-done(((bf16[8,128,512]{1,2,0:T(8,128)(2,1)}), bf16[8,128,512]{1,2,0:T(8,128)(2,1)S(1)}, u32[]{:S(2)}, u32[]{:S(2)}) %all-to-all-start.5) | async-done | bytes 1048608 | tf_op jit(solution)/shard_map/all_to_all | solution.py:74
  212.4 3.6 %all-to-all-start.3 = ((bf16[8,256,512]{1,2,0:T(8,128)(2,1)}), bf16[8,256,512]{1,2,0:T(8,128)(2,1)S(1)}, u32[]{:S(2)}, u32[]{:S(2)}) async-start(bf16[8,256,512]{1,2,0:T(8,128)(2,1)} %fusion), calls=%async_computation.3 | async-start | bytes 4194304 | tf_op jit(solution)/shard_map/all_to_all | solution.py:74
  216.0 4.2 %fusion.8 = f32[512,8,128]{2,0,1:T(8,128)S(1)} fusion(bf16[8,1536,128]{2,1,0:T(8,128)(2,1)} %bitcast.67, bf16[1536,512]{1,0:T(8,128)(2,1)} %get-tuple-element.22), kind=kOutput, calls=%fused_computation.19 | convolution fusion | flops 1610612736 | bytes 6815744 | tf_op jit(solution)/shard_map/dot_general | solution.py:67
  220.2 2.8 fusion.2
  222.9 23.3 %all-to-all-done.3 = bf16[8,256,512]{1,2,0:T(8,128)(2,1)S(1)} async-done(((bf16[8,256,512]{1,2,0:T(8,128)(2,1)}), bf16[8,256,512]{1,2,0:T(8,128)(2,1)S(1)}, u32[]{:S(2)}, u32[]{:S(2)}) %all-to-all-start.3) | async-done | bytes 2097184 | tf_op jit(solution)/shard_map/all_to_all | solution.py:74
  246.3 4.2 %all-to-all-start.4 = ((bf16[8,128,512]{1,2,0:T(8,128)(2,1)}), bf16[8,128,512]{1,2,0:T(8,128)(2,1)}, u32[]{:S(2)}, u32[]{:S(2)}) async-start(bf16[8,128,512]{1,2,0:T(8,128)(2,1)} %fusion.2), calls=%async_computation.4 | async-start | bytes 2097152 | tf_op jit(solution)/shard_map/all_to_all | solution.py:74
  250.5 1.1 convert_reduce_fusion
  251.6 3.8 %collective-permute-start.4 = (f32[256,512]{0,1:T(8,128)}, f32[256,512]{0,1:T(8,128)S(1)}, u32[]{:S(2)}, u32[]{:S(2)}) collective-permute-start(f32[256,512]{0,1:T(8,128)} %convert_reduce_fusion), channel_id=1, source_target_pairs={{0,0},{1,16},{16,1},{17,17},{2,2},{3,18},{18,3},{19,19},{4,4},{5,2... | collective-permute-start | bytes 1572872 | tf_op jit(solution)/shard_map/ppermute | solution.py:76
  255.4 0.1 convert_reduce_fusion.1
  255.5 1.9 collective-permute-start.8
  257.5 8.4 %all-to-all-done.4 = bf16[8,128,512]{1,2,0:T(8,128)(2,1)} async-done(((bf16[8,128,512]{1,2,0:T(8,128)(2,1)}), bf16[8,128,512]{1,2,0:T(8,128)(2,1)}, u32[]{:S(2)}, u32[]{:S(2)}) %all-to-all-start.4) | async-done | bytes 1048608 | tf_op jit(solution)/shard_map/all_to_all | solution.py:74
  265.9 1.4 convert_reduce_fusion.2
  267.3 3.5 %collective-permute-start.6 = (f32[128,512]{0,1:T(8,128)S(1)}, f32[128,512]{0,1:T(8,128)S(1)}, u32[]{:S(2)}, u32[]{:S(2)}) collective-permute-start(f32[128,512]{0,1:T(8,128)S(1)} %convert_reduce_fusion.2), channel_id=1, source_target_pairs={{0,0},{1,16},{16,1},{17,17},{2,2},{3,18},{18,3},{19,19},{4,4},{5,2... | collective-permute-start | bytes 786440 | tf_op jit(solution)/shard_map/ppermute | solution.py:76
  270.8 0.8 collective-permute-done.8
  271.6 3.3 %collective-permute-done.6 = f32[128,512]{0,1:T(8,128)S(1)} collective-permute-done((f32[128,512]{0,1:T(8,128)S(1)}, f32[128,512]{0,1:T(8,128)S(1)}, u32[]{:S(2)}, u32[]{:S(2)}) %collective-permute-start.6) | collective-permute-done | bytes 262176 | tf_op jit(solution)/shard_map/ppermute | solution.py:76
  275.0 0.1 pad_maximum_fusion
  275.1 1.3 copy.36
  (29 shorter events, 0.2 us)
Async XLA Ops:
  7.2 3.4 %copy-start = (f32[512]{0:T(512)S(1)}, f32[512]{0:T(512)}, u32[]{:S(2)}) copy-start(f32[512]{0:T(512)} %param.7) | copy-start | bytes 6148
  7.2 2.3 copy-start.1
  7.2 82.1 %all-gather.7.cloned.1.call-start = ((), (), s32[]{:S(2)}) async-start(), calls=%async_computation.6 | async-start | bytes 7077888 | tf_op jit(solution)/shard_map/all_gather | solution.py:31
  9.4 4.7 %copy-start.8 = (s32[1,12]{1,0:T(1,128)S(1)}, s32[1,12]{1,0:T(1,128)}, u32[]{:S(2)}) copy-start(s32[1,12]{1,0:T(1,128)} %param.9) | copy-start | bytes 148
  9.4 16.1 %copy-start.6 = (s32[1,1536]{1,0:T(1,128)S(1)}, s32[1,1536]{1,0:T(1,128)}, u32[]{:S(2)}) copy-start(s32[1,1536]{1,0:T(1,128)} %param.8) | copy-start | bytes 18436
  9.5 21.9 %copy-start.5 = (f32[1536]{0:T(1024)S(1)}, f32[1536]{0:T(1024)}, u32[]{:S(2)}) copy-start(f32[1536]{0:T(1024)} %param.6) | copy-start | bytes 18436
  9.5 124.5 %all-gather.11.cloned.1.call-start = ((), (), s32[]{:S(2)}) async-start(), calls=%async_computation.8 | async-start | bytes 3538944 | tf_op jit(solution)/shard_map/all_gather | solution.py:31
  10.5 168.9 %all-gather.9.cloned.1.call-start = ((), (), s32[]{:S(2)}) async-start(), calls=%async_computation.7 | async-start | bytes 3538944 | tf_op jit(solution)/shard_map/all_gather | solution.py:31
  11.9 3.2 %collective-permute-start = (f32[1536]{0:T(1024)S(1)}, f32[1536]{0:T(1024)S(1)}, u32[]{:S(2)}, u32[]{:S(2)}) collective-permute-start(f32[1536]{0:T(1024)S(1)} %convolution_reduce_fusion), channel_id=1, source_target_pairs={{0,1},{1,0},{2,3},{3,2},{4,5},{5,4},{6,7},{7,6},{8,9},{9,8},{10,11... | collective-permute-start | bytes 18440 | tf_op jit(solution)/shard_map/ppermute | solution.py:34
  15.8 15.5 %all-to-all-start = ((f32[8,1,1536]{2,1,0:T(1,128)}), f32[8,1,1536]{2,1,0:T(1,128)S(1)}, u32[]{:S(2)}, u32[]{:S(2)}) async-start(f32[8,1,1536]{2,1,0:T(1,128)} %broadcast_in_dim.9), calls=%async_computation | async-start | bytes 98304 | tf_op jit(solution)/shard_map/all_to_all | solution.py:23
  24.2 54.9 %collective-permute-start.1 = (bf16[1536,512]{1,0:T(8,128)(2,1)S(1)}, bf16[1536,512]{1,0:T(8,128)(2,1)S(1)}, u32[]{:S(2)}, u32[]{:S(2)}) collective-permute-start(bf16[1536,512]{1,0:T(8,128)(2,1)S(1)} %copy-done.1), channel_id=1, source_target_pairs={{0,1},{1,0},{2,3},{3,2},{4,5},{5,4},{6,7},{7,6},{8,9},{9,8},{10,11... | collective-permute-start | bytes 4718600 | tf_op jit(solution)/shard_map/ppermute | solution.py:35
  65.7 1.4 collective-permute-start.2
  67.8 10.7 %all-to-all-start.2 = ((f32[8,1,512]{2,1,0:T(1,128)}), f32[8,1,512]{2,1,0:T(1,128)S(1)}, u32[]{:S(2)}, u32[]{:S(2)}) async-start(f32[8,1,512]{2,1,0:T(1,128)} %broadcast_in_dim.11), calls=%async_computation.2 | async-start | bytes 32768 | tf_op jit(solution)/shard_map/all_to_all | solution.py:23
  89.3 44.7 %copy-start.4 = (bf16[1536,512]{1,0:T(8,128)(2,1)S(1)}, bf16[1536,512]{1,0:T(8,128)(2,1)}, u32[]{:S(2)}) copy-start(bf16[1536,512]{1,0:T(8,128)(2,1)} %get-tuple-element.5) | copy-start | bytes 4718596
  98.2 97.7 %collective-permute-start.3 = (f32[8,256,512]{1,2,0:T(8,128)}, f32[8,256,512]{1,2,0:T(8,128)}, u32[]{:S(2)}, u32[]{:S(2)}) collective-permute-start(f32[8,256,512]{1,2,0:T(8,128)} %convolution_bitcast_fusion), channel_id=1, source_target_pairs={{0,16},{16,0},{1,17},{17,1},{2,18},{18,2},{3,19},{19,3},{4,20},{20... | collective-permute-start | bytes 12582920 | tf_op jit(solution)/shard_map/ppermute | solution.py:72
  139.1 49.1 %collective-permute-start.7 = (f32[8,128,512]{1,2,0:T(8,128)}, f32[8,128,512]{1,2,0:T(8,128)S(1)}, u32[]{:S(2)}, u32[]{:S(2)}) collective-permute-start(f32[8,128,512]{1,2,0:T(8,128)} %convolution_bitcast_fusion.1), channel_id=1, source_target_pairs={{0,16},{16,0},{1,17},{17,1},{2,18},{18,2},{3,19},{19,3},{4,20},{20... | collective-permute-start | bytes 6291464 | tf_op jit(solution)/shard_map/ppermute | solution.py:72
  179.4 6.9 %copy-start.2 = (bf16[1536,512]{1,0:T(8,128)(2,1)S(1)}, bf16[1536,512]{1,0:T(8,128)(2,1)}, u32[]{:S(2)}) copy-start(bf16[1536,512]{1,0:T(8,128)(2,1)} %get-tuple-element.22) | copy-start | bytes 4718596
  179.4 6.9 %copy-start.7 = (bf16[12288,128]{1,0:T(8,128)(2,1)S(1)}, bf16[12288,128]{1,0:T(8,128)(2,1)}, u32[]{:S(2)}) copy-start(bf16[12288,128]{1,0:T(8,128)(2,1)} %all-gather.11.cloned.1.call-done) | copy-start | bytes 9437188
  185.1 35.1 %collective-permute-start.5 = (f32[8,128,512]{1,2,0:T(8,128)}, f32[8,128,512]{1,2,0:T(8,128)}, u32[]{:S(2)}, u32[]{:S(2)}) collective-permute-start(f32[8,128,512]{1,2,0:T(8,128)} %convolution_bitcast_fusion.2), channel_id=1, source_target_pairs={{0,16},{16,0},{1,17},{17,1},{2,18},{18,2},{3,19},{19,3},{4,20},{20... | collective-permute-start | bytes 6291464 | tf_op jit(solution)/shard_map/ppermute | solution.py:72
  189.3 6.6 %copy-start.3 = (bf16[1536,512]{1,0:T(8,128)(2,1)S(1)}, bf16[1536,512]{1,0:T(8,128)(2,1)}, u32[]{:S(2)}) copy-start(bf16[1536,512]{1,0:T(8,128)(2,1)} %get-tuple-element.22) | copy-start | bytes 4718596
  189.3 23.0 %all-to-all-start.5 = ((bf16[8,128,512]{1,2,0:T(8,128)(2,1)}), bf16[8,128,512]{1,2,0:T(8,128)(2,1)S(1)}, u32[]{:S(2)}, u32[]{:S(2)}) async-start(bf16[8,128,512]{1,2,0:T(8,128)(2,1)} %fusion.1), calls=%async_computation.5 | async-start | bytes 2097152 | tf_op jit(solution)/shard_map/all_to_all | solution.py:74
  212.4 33.9 %all-to-all-start.3 = ((bf16[8,256,512]{1,2,0:T(8,128)(2,1)}), bf16[8,256,512]{1,2,0:T(8,128)(2,1)S(1)}, u32[]{:S(2)}, u32[]{:S(2)}) async-start(bf16[8,256,512]{1,2,0:T(8,128)(2,1)} %fusion), calls=%async_computation.3 | async-start | bytes 4194304 | tf_op jit(solution)/shard_map/all_to_all | solution.py:74
  246.3 19.6 %all-to-all-start.4 = ((bf16[8,128,512]{1,2,0:T(8,128)(2,1)}), bf16[8,128,512]{1,2,0:T(8,128)(2,1)}, u32[]{:S(2)}, u32[]{:S(2)}) async-start(bf16[8,128,512]{1,2,0:T(8,128)(2,1)} %fusion.2), calls=%async_computation.4 | async-start | bytes 2097152 | tf_op jit(solution)/shard_map/all_to_all | solution.py:74
  251.6 23.3 %collective-permute-start.4 = (f32[256,512]{0,1:T(8,128)}, f32[256,512]{0,1:T(8,128)S(1)}, u32[]{:S(2)}, u32[]{:S(2)}) collective-permute-start(f32[256,512]{0,1:T(8,128)} %convert_reduce_fusion), channel_id=1, source_target_pairs={{0,0},{1,16},{16,1},{17,17},{2,2},{3,18},{18,3},{19,19},{4,4},{5,2... | collective-permute-start | bytes 1572872 | tf_op jit(solution)/shard_map/ppermute | solution.py:76
  255.5 16.1 %collective-permute-start.8 = (f32[128,512]{0,1:T(8,128)S(1)}, f32[128,512]{0,1:T(8,128)S(1)}, u32[]{:S(2)}, u32[]{:S(2)}) collective-permute-start(f32[128,512]{0,1:T(8,128)S(1)} %convert_reduce_fusion.1), channel_id=1, source_target_pairs={{0,0},{1,16},{16,1},{17,17},{2,2},{3,18},{18,3},{19,19},{4,4},{5,2... | collective-permute-start | bytes 786440 | tf_op jit(solution)/shard_map/ppermute | solution.py:76
  267.3 7.7 %collective-permute-start.6 = (f32[128,512]{0,1:T(8,128)S(1)}, f32[128,512]{0,1:T(8,128)S(1)}, u32[]{:S(2)}, u32[]{:S(2)}) collective-permute-start(f32[128,512]{0,1:T(8,128)S(1)} %convert_reduce_fusion.2), channel_id=1, source_target_pairs={{0,0},{1,16},{16,1},{17,17},{2,2},{3,18},{18,3},{19,19},{4,4},{5,2... | collective-permute-start | bytes 786440 | tf_op jit(solution)/shard_map/ppermute | solution.py:76
Sparse Core Ops, SparseCore 0:
  10.4 78.8 all-gather.6
  91.0 42.8 all-gather.10
  135.8 43.5 all-gather.8

commit v3 on v2

--- a/solution.py
+++ b/solution.py
@@ -1,16 +1,18 @@
 import jax
 import jax.numpy as jnp
 from jax import lax
+from jax.experimental import pallas as pl
+from jax.experimental.pallas import tpu as pltpu
 from jax.sharding import Mesh
 from jax.sharding import PartitionSpec as P
 
 ARCS_DEV = 4
 ARCS = ("x", "yh", "core")
 TILES = ("z", "yl")
-WIDTHS = (256, 128, 128)
-PAIR = [(0, 1), (1, 0)]
+FIRST, WIDTH = 256, 128
 prior_rows = 4.0
 f32, bf16 = jnp.float32, jnp.bfloat16
+PAIR = [(0, 1), (1, 0)]
 
 
 def after(array, *first):
@@ -23,18 +25,74 @@
     return lax.all_to_all(sent, axis, 0, 0, tiled=True).sum(axis=0)
 
 
+def product(place, blocks, right, added=None):
+    count, (rows, width), cols = len(blocks), blocks[0].shape, right.shape[1]
+    dtype = f32 if added is None else bf16
+
+    def kernel(place_ref, *refs):
+        right_ref, out_ref = refs[count], refs[-1]
+        for i in range(count):
+            part = lax.dot_general(
+                refs[i][...],
+                right_ref[...],
+                (((0,), (0,)), ((), ())),
+                preferred_element_type=f32,
+            )
+            at = place_ref[i]
+            if added is not None:
+                part = part + refs[count + 1][at]
+            out_ref[at] = part.astype(dtype)
+
+    extra = [] if added is None else [added]
+    vmem = pl.BlockSpec(memory_space=pltpu.VMEM)
+    return pl.pallas_call(
+        kernel,
+        out_shape=jax.ShapeDtypeStruct((count, width, cols), dtype),
+        in_specs=[pl.BlockSpec(memory_space=pltpu.SMEM)] + [vmem] * (count + 1 + len(extra)),
+        out_specs=vmem,
+        cost_estimate=pl.CostEstimate(
+            flops=2 * count * rows * width * cols,
+            bytes_accessed=2 * count * rows * width + 2 * rows * cols + 4 * count * width * cols,
+            transcendentals=0,
+        ),
+    )(place, *blocks, right, *extra)
+
+
 def local(design, observations, solution, arc_ids, block_live):
     rows, _ = design.shape
-    core, yl = lax.axis_index("core"), lax.axis_index("yl")
-    gathered, begin = [], 0
-    for width in WIDTHS:
-        gathered.append(lax.all_gather(design[:, begin : begin + width], "z", axis=0))
-        begin += width
+    core, yl, z = lax.axis_index("core"), lax.axis_index("yl"), lax.axis_index("z")
+    n = lax.axis_size("z")
+    up = [(i, (i + 1) % n) for i in range(n)]
+    down = [(i, (i - 1) % n) for i in range(n)]
+
+    gathered = lax.all_gather(design[:, :FIRST], "z", axis=0)
+    last = lax.all_gather(design[:, FIRST + WIDTH :], "z", axis=0)
+
+    def start(begin, flip, *tied):
+        own = design[:, begin : begin + WIDTH]
+        own = after(own, *tied) if tied else own
+        return {"ends": [own, own], "blocks": [own], "steps": [0], "flip": flip}
+
+    def hop(ring):
+        d = (len(ring["blocks"]) + 1) // 2
+        for side in range(2 if d < n // 2 else 1):
+            way = up if side == ring["flip"] else down
+            end = lax.ppermute(ring["ends"][side], "z", way)
+            ring["ends"][side] = end
+            ring["blocks"].append(end)
+            ring["steps"].append(-d if way is up else d)
+        return ring["blocks"][-2:]
+
+    def stacked(ring):
+        return lax.rem(z + n + jnp.array(ring["steps"], jnp.int32), n), ring["blocks"]
+
+    early = start(FIRST, 0)
+    hops = [hop(early) for _ in range(n // 2)]
     partial_value = jnp.dot(design.astype(f32), solution, precision=lax.Precision.HIGHEST)
     from_pair = lax.ppermute(partial_value, "yl", PAIR)
     other = lax.ppermute(after(design, from_pair), "yl", PAIR)
     predicted = of_everyone(partial_value + from_pair, "z")
-    residual = observations - predicted
+    residual = after(observations - predicted, *hops[0])
     live_row = (
         jnp.broadcast_to(block_live[0][:, None], (block_live.shape[1], 128))
         .reshape(rows)
@@ -49,6 +107,7 @@
     arc_weight = variance_all / (
         (arc_squares + prior_rows * variance_all) / (arc_counts + prior_rows)
     )
+    arc_weight = after(arc_weight, *hops[1])
     row_weight = live_row * jnp.sum(arc_match * arc_weight[:, None], axis=0)
     rhs_part = lax.dot_general(
         design.astype(f32),
@@ -63,17 +122,27 @@
     mine = jnp.where(core == yl, weighted_own, weighted_other)
     theirs = jnp.where(core == yl, weighted_other, weighted_own)
 
-    def product(left, right):
-        return lax.dot_general(left, right, (((1,), (0,)), ((), ())), preferred_element_type=f32)
+    def share(left, right, added=None):
+        if isinstance(left, tuple):
+            return product(*left, right, added)
+        out = lax.dot_general(left, right, (((1,), (0,)), ((), ())), preferred_element_type=f32)
+        return out if added is None else (out + added).astype(bf16)
 
-    done, swap = [], [(0, 0), (1, 2), (2, 1), (3, 3)]
-    for j, left in enumerate(gathered):
-        sent = product(left, theirs if j else after(theirs, rhs))
-        from_core = lax.ppermute(sent, "core", PAIR)
-        pair = (product(left, mine) + from_core).astype(bf16)
+    def spread(pair):
         got = lax.all_to_all(pair, ("x", "yh"), 0, 0, tiled=True)
         block = jnp.sum(got.astype(f32), axis=0)
-        done.append(lax.ppermute(block, ("core", "yl"), swap))
+        return lax.ppermute(block, ("core", "yl"), [(0, 0), (1, 2), (2, 1), (3, 3)])
+
+    def whole_chunk(left, *tied):
+        sent = share(left, after(theirs, *tied) if tied else theirs)
+        from_core = lax.ppermute(sent, "core", PAIR)
+        return share(left, mine, from_core)
+
+    pair_r = whole_chunk(stacked(early))
+    hopped = spread(pair_r)
+    pair_a = whole_chunk(gathered, pair_r)
+    first = spread(pair_a)
+    done = [first, hopped, spread(whole_chunk(last))]
     return jnp.concatenate(done, axis=0), rhs
 
 

time: 284 us -> 258 us (0.908)
  waiting for transfers between devices: 140 us -> 106 us
  blocking collectives: 29.4 us -> 10.9 us
  starting transfers between devices: 43.6 us -> 57.6 us
  Pallas kernels: 0 us -> 11.6 us
  matrix products: 35.8 us -> 27 us
  other arithmetic: 12.1 us -> 18.5 us
  local copies, waits for them, and re-layouts: 6.42 us -> 9.5 us
    all_gather x3 -> x2, waiting for transfers between devices: 81.9 us -> 21.9 us  [the longest x1 21.9 us: local(): last = lax.all_gather(design[:, FIRST + WIDTH:], 'z', axis=0)]
    ppermute x6 -> x13, waiting for transfers between devices: 4.18 us -> 36.8 us  [the longest x7 32.7 us: hop(): end = lax.ppermute(ring['ends'][side], 'z', way)]
    all_to_all x1, blocking collectives: 29.4 us -> 10.9 us  [of_everyone(): return lax.all_to_all(sent, axis, 0, 0, tiled=True).sum(axis=0)]
    pallas_call x0 -> x2, Pallas kernels: none -> 11.6 us  [product(): pl.pallas_call(kernel, out_shape=jax.ShapeDtypeStruct((count, width, cols...]
    ppermute x6 -> x13, starting transfers between devices: 12.4 us -> 24 us  [the longest x7 11.8 us: hop(): end = lax.ppermute(ring['ends'][side], 'z', way)]
    all_to_all x3, waiting for transfers between devices: 40.1 us -> 30.6 us  [spread(): got = lax.all_to_all(pair, ('x', 'yh'), 0, 0, tiled=True)]
    dot_general x6 -> x4, matrix products: 33.7 us -> 25 us  [share(): lax.dot_general(left, right, (((1,), (0,)), ((), ())), preferred_element_...]
    all_to_all x2, starting transfers between devices: 12.5 us -> 16.4 us  [of_everyone(): return lax.all_to_all(sent, axis, 0, 0, tiled=True).sum(axis=0)]
  transfers between devices with their start and end apart: 17 -> 23, of which waited for: 12 -> 10; matrix products, arithmetic and copies ran while one was open for 18% -> 19% of each run, Pallas kernels for 0% -> 5%
where the time goes in v3:
time: 258 us; the launch traced here: 257 us
  waiting for transfers between devices  106 us (41%)
  starting transfers between devices  57.6 us (22%)
  matrix products  27 us (10%)
  other arithmetic  18.5 us (7%)
  between operations  15.6 us (6%)
  Pallas kernels  11.6 us (4%)
  blocking collectives  10.9 us (4%)
  local copies, waits for them, and re-layouts  9.5 us (4%)
    ppermute x7, waiting for transfers between devices, hop(): end = lax.ppermute(ring['ends'][side], 'z', way)  32.7 us
    all_to_all x3, waiting for transfers between devices, spread(): got = lax.all_to_all(pair, ('x', 'yh'), 0, 0, tiled=True)  30.6 us
    dot_general x4, matrix products, share(): lax.dot_general(left, right, (((1,), (0,)), ((), ())), preferred_element_...  25 us
    all_gather x1, waiting for transfers between devices, local(): last = lax.all_gather(design[:, FIRST + WIDTH:], 'z', axis=0)  21.9 us
    all_to_all x2, starting transfers between devices, of_everyone(): return lax.all_to_all(sent, axis, 0, 0, tiled=True).sum(axis=0)  16.4 us
    all_to_all x3, starting transfers between devices, spread(): got = lax.all_to_all(pair, ('x', 'yh'), 0, 0, tiled=True)  14.5 us
    all_to_all x2, waiting for transfers between devices, of_everyone(): return lax.all_to_all(sent, axis, 0, 0, tiled=True).sum(axis=0)  14.2 us
    ppermute x7, starting transfers between devices, hop(): end = lax.ppermute(ring['ends'][side], 'z', way)  11.8 us
  transfers between devices with their start and end apart: 23, of which 10 were waited for; matrix products, arithmetic and copies ran while one was open for 19% of the time, Pallas kernels for 5%

profile of v3, /device:TPU:1, one launch (start us, length us, event | category | flops | bytes accessed | tf_op | source)
XLA Modules:
  0.0 257.0 jit_solution(3860629264160861870)
XLA Ops:
  7.2 0.0 all-gather.5.cloned.1.call-start
  7.2 2.2 slice.18
  9.5 0.8 fusion.9
  10.3 2.5 collective-permute-start.1
  12.8 3.9 %collective-permute-start.2 = (bf16[1536,128]{1,0:T(8,128)(2,1)S(1)}, bf16[1536,128]{1,0:T(8,128)(2,1)S(1)}, u32[]{:S(2)}, u32[]{:S(2)}) collective-permute-start(bf16[1536,128]{1,0:T(8,128)(2,1)S(1)} %get-tuple-element.28.refs_0_), channel_id=1, source_target_pairs={{0,14},{2,0},{4,2},{6,4},{8,6},{10,8},{12,10},{14,12},{1,15},{3,1}... | collective-permute-start | bytes 1179656 | tf_op jit(solution)/shard_map/ppermute | solution.py:80
  16.7 1.3 convolution_reduce_fusion
  18.1 1.4 collective-permute-start
  19.4 1.5 collective-permute-done
  20.9 1.3 collective-permute-start.5
  22.2 0.7 broadcast_bitcast_fusion
  22.9 0.6 broadcast_in_dim.9
  23.6 5.3 %all-to-all-start = ((f32[8,1,1536]{2,1,0:T(1,128)}), f32[8,1,1536]{2,1,0:T(1,128)S(1)}, u32[]{:S(2)}, u32[]{:S(2)}) async-start(f32[8,1,1536]{2,1,0:T(1,128)} %broadcast_in_dim.9), calls=%async_computation | async-start | bytes 98304 | tf_op jit(solution)/shard_map/all_to_all | solution.py:25
  28.8 0.6 compare_select_fusion.place_ref
  29.5 7.1 %all-to-all-done = f32[8,1,1536]{2,1,0:T(1,128)S(1)} async-done(((f32[8,1,1536]{2,1,0:T(1,128)}), f32[8,1,1536]{2,1,0:T(1,128)S(1)}, u32[]{:S(2)}, u32[]{:S(2)}) %all-to-all-start) | async-done | bytes 49184 | tf_op jit(solution)/shard_map/all_to_all | solution.py:25
  36.7 0.4 collective-permute-start.3
  37.0 0.2 copy-done.13
  37.2 0.1 multiply_multiply_fusion
  37.3 2.2 collective-permute-start.4
  39.5 1.5 select_reduce_fusion.3
  41.0 1.4 pad_maximum_fusion.1
  42.3 0.6 broadcast_in_dim.10
  42.9 11.1 %all-to-all-start.1 = ((f32[16,1,2]{2,1,0:T(1,128)}), f32[16,1,2]{2,1,0:T(1,128)}, u32[]{:S(2)}, u32[]{:S(2)}) async-start(f32[16,1,2]{2,1,0:T(1,128)} %broadcast_in_dim.10), calls=%async_computation.1 | async-start | bytes 16384 | tf_op jit(solution)/shard_map/all_to_all | solution.py:25
  54.1 7.1 %all-to-all-done.1 = f32[16,1,2]{2,1,0:T(1,128)} async-done(((f32[16,1,2]{2,1,0:T(1,128)}), f32[16,1,2]{2,1,0:T(1,128)}, u32[]{:S(2)}, u32[]{:S(2)}) %all-to-all-start.1) | async-done | bytes 160 | tf_op jit(solution)/shard_map/all_to_all | solution.py:25
  61.2 1.2 reduce_sum.102
  62.4 1.4 fusion.10
  65.1 0.1 collective-permute-start.6
  65.2 0.7 add_divide_fusion
  65.9 2.7 %collective-permute-start.7 = (bf16[1536,128]{1,0:T(8,128)(2,1)S(1)}, bf16[1536,128]{1,0:T(8,128)(2,1)S(1)}, u32[]{:S(2)}, u32[]{:S(2)}) collective-permute-start(bf16[1536,128]{1,0:T(8,128)(2,1)S(1)} %collective-permute-done.4.refs_4_), channel_id=1, source_target_pairs={{0,14},{2,0},{4,2},{6,4},{8,6},{10,8},{12,10},{14,12},{1,15},{3,1}... | collective-permute-start | bytes 1179656 | tf_op jit(solution)/shard_map/ppermute | solution.py:80
  68.6 0.1 select_reduce_fusion.4
  68.7 0.8 fusion.8
  69.5 16.4 %collective-permute-done.6.refs_5_ = bf16[1536,128]{1,0:T(8,128)(2,1)S(1)} collective-permute-done((bf16[1536,128]{1,0:T(8,128)(2,1)S(1)}, bf16[1536,128]{1,0:T(8,128)(2,1)S(1)}, u32[]{:S(2)}, u32[]{:S(2)}) %collective-permute-start.6) | collective-permute-done | bytes 393248 | tf_op jit(solution)/shard_map/ppermute | solution.py:80
  85.9 4.1 %broadcast_select_fusion.1 = (bf16[1536,512]{1,0:T(8,128)(2,1)}, bf16[1536,512]{1,0:T(8,128)(2,1)}) fusion(pred[]{:T(512)S(6)} %eq.19, bf16[1536,512]{1,0:T(8,128)(2,1)S(1)} %copy-done.1, f32[1536]{0:T(1024)S(1)} %get-tuple-element.25, bf16[1536,512]{1,0:T(8,128)(2,1)} %collective-permute-done.5), kind=kLoop, calls=%fused_computation.17 | loop fusion | flops 6291456 | bytes 6297601 | tf_op jit(solution)/shard_map/jit(_where)/select_n | solution.py:122
  90.1 16.3 %collective-permute-done.8.refs_7_ = bf16[1536,128]{1,0:T(8,128)(2,1)S(1)} collective-permute-done((bf16[1536,128]{1,0:T(8,128)(2,1)S(1)}, bf16[1536,128]{1,0:T(8,128)(2,1)S(1)}, u32[]{:S(2)}, u32[]{:S(2)}) %collective-permute-start.8) | collective-permute-done | bytes 393248 | tf_op jit(solution)/shard_map/ppermute | solution.py:80
  106.4 0.7 copy-done.12
  107.2 5.6 %shard_map.77 = f32[8,128,512]{2,1,0:T(8,128)} custom-call(s32[8]{0:T(128)} %compare_select_fusion.place_ref, bf16[1536,128]{1,0:T(8,128)(2,1)} %copy-done.5, bf16[1536,128]{1,0:T(8,128)(2,1)} %copy-done.6, bf16[1536,128]{1,0:T(8,128)(2,1)} %copy-done.7, bf16[1536,128]{1,0:T(8,128)(2,1)} %copy-done.8, bf16[1536,128]{1,0:T(8,128)(2,1)} %copy-done.9, ...), custom_call_target="tpu_custom_call" | custom-call | flops 1610612736 | bytes 6815744 | tf_op jit(solution)/shard_map/pallas_call | solution.py:48
  112.7 1.8 collective-permute-start.9
  114.5 4.1 %collective-permute-done.9.refs_9_ = f32[8,128,512]{2,1,0:T(8,128)} collective-permute-done((f32[8,128,512]{2,1,0:T(8,128)}, f32[8,128,512]{2,1,0:T(8,128)}, u32[]{:S(2)}, u32[]{:S(2)}) %collective-permute-start.9) | collective-permute-done | bytes 2097184 | tf_op jit(solution)/shard_map/ppermute | solution.py:138
  118.6 6.0 %shard_map.78 = bf16[8,128,512]{2,1,0:T(8,128)(2,1)} custom-call(s32[8]{0:T(128)} %compare_select_fusion.place_ref, bf16[1536,128]{1,0:T(8,128)(2,1)} %copy-done.5, bf16[1536,128]{1,0:T(8,128)(2,1)} %copy-done.6, bf16[1536,128]{1,0:T(8,128)(2,1)} %copy-done.7, bf16[1536,128]{1,0:T(8,128)(2,1)} %copy-done.8, bf16[1536,128]{1,0:T(8,128)(2,1)} %copy-done.9, ...), custom_call_target="tpu_custom_call" | custom-call | flops 1610612736 | bytes 6815744 | tf_op jit(solution)/shard_map/pallas_call | solution.py:48
  124.7 7.9 %convolution_bitcast_fusion = f32[8,256,512]{1,2,0:T(8,128)} fusion(bf16[8,1536,256]{2,1,0:T(8,128)(2,1)} %bitcast.48, bf16[1536,512]{1,0:T(8,128)(2,1)S(1)} %copy-done.2), kind=kOutput, calls=%fused_computation.5 | convolution fusion | flops 3221225472 | bytes 12058624 | tf_op jit(solution)/shard_map/dot_general | solution.py:128
  132.6 0.4 collective-permute-start.10
  133.0 4.3 %all-to-all-start.3 = ((bf16[8,128,512]{2,1,0:T(8,128)(2,1)}), bf16[8,128,512]{2,1,0:T(8,128)(2,1)}, u32[]{:S(2)}, u32[]{:S(2)}) async-start(bf16[8,128,512]{2,1,0:T(8,128)(2,1)} %shard_map.78), calls=%async_computation.3 | async-start | bytes 2097152 | tf_op jit(solution)/shard_map/all_to_all | solution.py:132
  137.2 21.9 %all-gather.7.cloned.1.call-done = bf16[12288,128]{1,0:T(8,128)(2,1)} async-done(((bf16[1536,128]{1,0:T(8,128)(2,1)}), bf16[12288,128]{1,0:T(8,128)(2,1)}) %all-gather.7.cloned.1.call-update) | async-done | bytes 3145744 | tf_op jit(solution)/shard_map/all_gather | solution.py:69
  159.2 5.2 %convolution_bitcast_fusion.1 = f32[8,128,512]{1,2,0:T(8,128)} fusion(bf16[8,1536,128]{2,1,0:T(8,128)(2,1)} %bitcast.50, bf16[1536,512]{1,0:T(8,128)(2,1)S(1)} %copy-done.2), kind=kOutput, calls=%fused_computation.10 | convolution fusion | flops 1610612736 | bytes 6815744 | tf_op jit(solution)/shard_map/dot_general | solution.py:128
  164.3 1.2 collective-permute-start.13
  165.6 8.1 %fusion = bf16[8,256,512]{1,2,0:T(8,128)(2,1)} fusion(f32[8,256,512]{1,2,0:T(8,128)} %collective-permute-done.10, bf16[8,1536,256]{2,1,0:T(8,128)(2,1)} %bitcast.49, bf16[1536,512]{1,0:T(8,128)(2,1)S(1)} %copy-done.3), kind=kOutput, calls=%fused_computation.1 | convolution fusion | flops 3223322624 | bytes 14155776 | tf_op jit(solution)/shard_map/dot_general | solution.py:128
  173.7 6.6 %all-to-all-start.2 = ((bf16[8,256,512]{1,2,0:T(8,128)(2,1)}), bf16[8,256,512]{1,2,0:T(8,128)(2,1)}, u32[]{:S(2)}, u32[]{:S(2)}) async-start(bf16[8,256,512]{1,2,0:T(8,128)(2,1)} %fusion), calls=%async_computation.2 | async-start | bytes 4194304 | tf_op jit(solution)/shard_map/all_to_all | solution.py:132
  180.2 3.7 %fusion.4 = f32[512,8,128]{2,0,1:T(8,128)S(1)} fusion(bf16[8,1536,128]{2,1,0:T(8,128)(2,1)} %bitcast.51, bf16[1536,512]{1,0:T(8,128)(2,1)S(1)} %copy-done.4), kind=kOutput, calls=%fused_computation.13 | convolution fusion | flops 1610612736 | bytes 6815744 | tf_op jit(solution)/shard_map/dot_general | solution.py:128
  184.0 2.8 %fusion.1 = bf16[8,128,512]{1,2,0:T(8,128)(2,1)} fusion(f32[8,128,512]{1,2,0:T(8,128)} %collective-permute-done.13, f32[512,8,128]{2,0,1:T(8,128)S(1)} %fusion.4), kind=kLoop, calls=%fused_computation.7 | loop fusion | flops 1048576 | bytes 5242880 | tf_op jit(solution)/shard_map/convert_element_type | solution.py:129
  186.8 24.8 %all-to-all-done.2 = bf16[8,256,512]{1,2,0:T(8,128)(2,1)} async-done(((bf16[8,256,512]{1,2,0:T(8,128)(2,1)}), bf16[8,256,512]{1,2,0:T(8,128)(2,1)}, u32[]{:S(2)}, u32[]{:S(2)}) %all-to-all-start.2) | async-done | bytes 2097184 | tf_op jit(solution)/shard_map/all_to_all | solution.py:132
  211.6 3.7 %all-to-all-start.4 = ((bf16[8,128,512]{1,2,0:T(8,128)(2,1)}), bf16[8,128,512]{1,2,0:T(8,128)(2,1)S(1)}, u32[]{:S(2)}, u32[]{:S(2)}) async-start(bf16[8,128,512]{1,2,0:T(8,128)(2,1)} %fusion.1), calls=%async_computation.4 | async-start | bytes 2097152 | tf_op jit(solution)/shard_map/all_to_all | solution.py:132
  215.3 1.9 convert_reduce_fusion
  217.2 3.5 %collective-permute-start.11 = (f32[256,512]{0,1:T(8,128)S(1)}, f32[256,512]{0,1:T(8,128)}, u32[]{:S(2)}, u32[]{:S(2)}) collective-permute-start(f32[256,512]{0,1:T(8,128)S(1)} %convert_reduce_fusion), channel_id=1, source_target_pairs={{0,0},{1,16},{16,1},{17,17},{2,2},{3,18},{18,3},{19,19},{4,4},{5,2... | collective-permute-start | bytes 1572872 | tf_op jit(solution)/shard_map/ppermute | solution.py:134
  220.7 1.4 convert_reduce_fusion.2
  222.1 0.8 copy.20
  223.0 2.0 collective-permute-start.12
  225.0 5.8 %all-to-all-done.4 = bf16[8,128,512]{1,2,0:T(8,128)(2,1)S(1)} async-done(((bf16[8,128,512]{1,2,0:T(8,128)(2,1)}), bf16[8,128,512]{1,2,0:T(8,128)(2,1)S(1)}, u32[]{:S(2)}, u32[]{:S(2)}) %all-to-all-start.4) | async-done | bytes 1048608 | tf_op jit(solution)/shard_map/all_to_all | solution.py:132
  230.8 0.1 convert_reduce_fusion.1
  231.0 3.3 %collective-permute-start.14 = (f32[128,512]{0,1:T(8,128)S(1)}, f32[128,512]{0,1:T(8,128)S(1)}, u32[]{:S(2)}, u32[]{:S(2)}) collective-permute-start(f32[128,512]{0,1:T(8,128)S(1)} %convert_reduce_fusion.1), channel_id=1, source_target_pairs={{0,0},{1,16},{16,1},{17,17},{2,2},{3,18},{18,3},{19,19},{4,4},{5,2... | collective-permute-start | bytes 786440 | tf_op jit(solution)/shard_map/ppermute | solution.py:134
  234.3 0.7 fusion.11
  235.0 1.2 collective-permute-done.15
  236.2 10.9 %all_to_all.33 = f32[8,1,512]{2,1,0:T(1,128)S(1)} all-to-all(f32[8,1,512]{2,1,0:T(1,128)S(1)} %broadcast_in_dim.11), channel_id=1, replica_groups=mesh['x'=4,'yh'=2,'core'=2,'z'=8,'yl'=2] {'x','yh'}, dimensions={0} | all-to-all | bytes 32768 | tf_op jit(solution)/shard_map/all_to_all | solution.py:25
  247.0 0.6 reduce_sum.109
  247.6 1.2 pad_maximum_fusion
  248.9 1.3 copy.22
  (60 shorter events, 0.3 us)
Async XLA Ops:
  7.2 9.6 %copy-start = (f32[512]{0:T(512)S(1)}, f32[512]{0:T(512)}, u32[]{:S(2)}) copy-start(f32[512]{0:T(512)} %param.8) | copy-start | bytes 6148
  7.2 2.3 copy-start.1
  7.2 117.5 %all-gather.5.cloned.1.call-start = ((), (), s32[]{:S(2)}) async-start(), calls=%async_computation.6 | async-start | bytes 7077888 | tf_op jit(solution)/shard_map/all_gather | solution.py:68
  9.4 10.0 %copy-start.16 = (s32[1,12]{1,0:T(1,128)S(1)}, s32[1,12]{1,0:T(1,128)}, u32[]{:S(2)}) copy-start(s32[1,12]{1,0:T(1,128)} %param.10) | copy-start | bytes 148
  9.4 19.4 %copy-start.17 = (s32[8]{0:T(128)S(1)}, s32[8]{0:T(128)}, u32[]{:S(2)}) copy-start(s32[8]{0:T(128)} %constant.33.clone) | copy-start | bytes 100
  9.4 20.0 %copy-start.15 = (s32[1,1536]{1,0:T(1,128)S(1)}, s32[1,1536]{1,0:T(1,128)}, u32[]{:S(2)}) copy-start(s32[1,1536]{1,0:T(1,128)} %param.9) | copy-start | bytes 18436
  9.5 27.1 %copy-start.14 = (f32[1536]{0:T(1024)S(1)}, f32[1536]{0:T(1024)}, u32[]{:S(2)}) copy-start(f32[1536]{0:T(1024)} %param.7) | copy-start | bytes 18436
  10.3 79.7 %copy-start.5 = (bf16[1536,128]{1,0:T(8,128)(2,1)}, bf16[1536,128]{1,0:T(8,128)(2,1)S(1)}, u32[]{:S(2)}) copy-start(bf16[1536,128]{1,0:T(8,128)(2,1)S(1)} %get-tuple-element.28.refs_0_) | copy-start | bytes 1179652
  10.3 26.3 %collective-permute-start.1 = (bf16[1536,128]{1,0:T(8,128)(2,1)S(1)}, bf16[1536,128]{1,0:T(8,128)(2,1)S(1)}, u32[]{:S(2)}, u32[]{:S(2)}) collective-permute-start(bf16[1536,128]{1,0:T(8,128)(2,1)S(1)} %get-tuple-element.28.refs_0_), channel_id=1, source_target_pairs={{0,2},{2,4},{4,6},{6,8},{8,10},{10,12},{12,14},{14,0},{1,3},{3,5},... | collective-permute-start | bytes 1179656 | tf_op jit(solution)/shard_map/ppermute | solution.py:80
  12.8 23.9 %collective-permute-start.2 = (bf16[1536,128]{1,0:T(8,128)(2,1)S(1)}, bf16[1536,128]{1,0:T(8,128)(2,1)S(1)}, u32[]{:S(2)}, u32[]{:S(2)}) collective-permute-start(bf16[1536,128]{1,0:T(8,128)(2,1)S(1)} %get-tuple-element.28.refs_0_), channel_id=1, source_target_pairs={{0,14},{2,0},{4,2},{6,4},{8,6},{10,8},{12,10},{14,12},{1,15},{3,1}... | collective-permute-start | bytes 1179656 | tf_op jit(solution)/shard_map/ppermute | solution.py:80
  18.1 2.9 %collective-permute-start = (f32[1536]{0:T(1024)S(1)}, f32[1536]{0:T(1024)S(1)}, u32[]{:S(2)}, u32[]{:S(2)}) collective-permute-start(f32[1536]{0:T(1024)S(1)} %convolution_reduce_fusion), channel_id=1, source_target_pairs={{0,1},{1,0},{2,3},{3,2},{4,5},{5,4},{6,7},{7,6},{8,9},{9,8},{10,11... | collective-permute-start | bytes 18440 | tf_op jit(solution)/shard_map/ppermute | solution.py:92
  20.9 65.0 %collective-permute-start.5 = (bf16[1536,512]{1,0:T(8,128)(2,1)S(1)}, bf16[1536,512]{1,0:T(8,128)(2,1)}, u32[]{:S(2)}, u32[]{:S(2)}) collective-permute-start(bf16[1536,512]{1,0:T(8,128)(2,1)S(1)} %copy-done.1), channel_id=1, source_target_pairs={{0,1},{1,0},{2,3},{3,2},{4,5},{5,4},{6,7},{7,6},{8,9},{9,8},{10,11... | collective-permute-start | bytes 4718600 | tf_op jit(solution)/shard_map/ppermute | solution.py:93
  23.6 13.0 %all-to-all-start = ((f32[8,1,1536]{2,1,0:T(1,128)}), f32[8,1,1536]{2,1,0:T(1,128)S(1)}, u32[]{:S(2)}, u32[]{:S(2)}) async-start(f32[8,1,1536]{2,1,0:T(1,128)} %broadcast_in_dim.9), calls=%async_computation | async-start | bytes 98304 | tf_op jit(solution)/shard_map/all_to_all | solution.py:25
  36.6 0.6 copy-start.13
  36.6 53.4 %copy-start.6 = (bf16[1536,128]{1,0:T(8,128)(2,1)}, bf16[1536,128]{1,0:T(8,128)(2,1)S(1)}, u32[]{:S(2)}) copy-start(bf16[1536,128]{1,0:T(8,128)(2,1)S(1)} %collective-permute-done.1.refs_1_) | copy-start | bytes 1179652
  36.7 53.4 %copy-start.7 = (bf16[1536,128]{1,0:T(8,128)(2,1)}, bf16[1536,128]{1,0:T(8,128)(2,1)S(1)}, u32[]{:S(2)}) copy-start(bf16[1536,128]{1,0:T(8,128)(2,1)S(1)} %collective-permute-done.2.refs_2_) | copy-start | bytes 1179652
  36.7 28.4 %collective-permute-start.3 = (bf16[1536,128]{1,0:T(8,128)(2,1)S(1)}, bf16[1536,128]{1,0:T(8,128)(2,1)S(1)}, u32[]{:S(2)}, u32[]{:S(2)}) collective-permute-start(bf16[1536,128]{1,0:T(8,128)(2,1)S(1)} %collective-permute-done.1.refs_1_), channel_id=1, source_target_pairs={{0,2},{2,4},{4,6},{6,8},{8,10},{10,12},{12,14},{14,0},{1,3},{3,5},... | collective-permute-start | bytes 1179656 | tf_op jit(solution)/shard_map/ppermute | solution.py:80
  37.3 28.6 %collective-permute-start.4 = (bf16[1536,128]{1,0:T(8,128)(2,1)S(1)}, bf16[1536,128]{1,0:T(8,128)(2,1)S(1)}, u32[]{:S(2)}, u32[]{:S(2)}) collective-permute-start(bf16[1536,128]{1,0:T(8,128)(2,1)S(1)} %collective-permute-done.2.refs_2_), channel_id=1, source_target_pairs={{0,14},{2,0},{4,2},{6,4},{8,6},{10,8},{12,10},{14,12},{1,15},{3,1}... | collective-permute-start | bytes 1179656 | tf_op jit(solution)/shard_map/ppermute | solution.py:80
  42.9 18.2 %all-to-all-start.1 = ((f32[16,1,2]{2,1,0:T(1,128)}), f32[16,1,2]{2,1,0:T(1,128)}, u32[]{:S(2)}, u32[]{:S(2)}) async-start(f32[16,1,2]{2,1,0:T(1,128)} %broadcast_in_dim.10), calls=%async_computation.1 | async-start | bytes 16384 | tf_op jit(solution)/shard_map/all_to_all | solution.py:25
  54.0 105.1 %all-gather.7.cloned.1.call-start = ((), (), s32[]{:S(2)}) async-start(), calls=%async_computation.7 | async-start | bytes 3538944 | tf_op jit(solution)/shard_map/all_gather | solution.py:69
  65.1 25.0 %copy-start.8 = (bf16[1536,128]{1,0:T(8,128)(2,1)}, bf16[1536,128]{1,0:T(8,128)(2,1)S(1)}, u32[]{:S(2)}) copy-start(bf16[1536,128]{1,0:T(8,128)(2,1)S(1)} %collective-permute-done.3.refs_3_) | copy-start | bytes 1179652
  65.1 20.8 %collective-permute-start.6 = (bf16[1536,128]{1,0:T(8,128)(2,1)S(1)}, bf16[1536,128]{1,0:T(8,128)(2,1)S(1)}, u32[]{:S(2)}, u32[]{:S(2)}) collective-permute-start(bf16[1536,128]{1,0:T(8,128)(2,1)S(1)} %collective-permute-done.3.refs_3_), channel_id=1, source_target_pairs={{0,2},{2,4},{4,6},{6,8},{8,10},{10,12},{12,14},{14,0},{1,3},{3,5},... | collective-permute-start | bytes 1179656 | tf_op jit(solution)/shard_map/ppermute | solution.py:80
  65.9 24.2 %copy-start.9 = (bf16[1536,128]{1,0:T(8,128)(2,1)}, bf16[1536,128]{1,0:T(8,128)(2,1)S(1)}, u32[]{:S(2)}) copy-start(bf16[1536,128]{1,0:T(8,128)(2,1)S(1)} %collective-permute-done.4.refs_4_) | copy-start | bytes 1179652
  65.9 24.2 %collective-permute-start.7 = (bf16[1536,128]{1,0:T(8,128)(2,1)S(1)}, bf16[1536,128]{1,0:T(8,128)(2,1)S(1)}, u32[]{:S(2)}, u32[]{:S(2)}) collective-permute-start(bf16[1536,128]{1,0:T(8,128)(2,1)S(1)} %collective-permute-done.4.refs_4_), channel_id=1, source_target_pairs={{0,14},{2,0},{4,2},{6,4},{8,6},{10,8},{12,10},{14,12},{1,15},{3,1}... | collective-permute-start | bytes 1179656 | tf_op jit(solution)/shard_map/ppermute | solution.py:80
  85.9 4.2 %copy-start.10 = (bf16[1536,128]{1,0:T(8,128)(2,1)}, bf16[1536,128]{1,0:T(8,128)(2,1)S(1)}, u32[]{:S(2)}) copy-start(bf16[1536,128]{1,0:T(8,128)(2,1)S(1)} %collective-permute-done.6.refs_5_) | copy-start | bytes 1179652
  85.9 20.5 %collective-permute-start.8 = (bf16[1536,128]{1,0:T(8,128)(2,1)S(1)}, bf16[1536,128]{1,0:T(8,128)(2,1)S(1)}, u32[]{:S(2)}, u32[]{:S(2)}) collective-permute-start(bf16[1536,128]{1,0:T(8,128)(2,1)S(1)} %collective-permute-done.6.refs_5_), channel_id=1, source_target_pairs={{0,2},{2,4},{4,6},{6,8},{8,10},{10,12},{12,14},{14,0},{1,3},{3,5},... | collective-permute-start | bytes 1179656 | tf_op jit(solution)/shard_map/ppermute | solution.py:80
  90.1 16.3 %copy-start.11 = (bf16[1536,128]{1,0:T(8,128)(2,1)}, bf16[1536,128]{1,0:T(8,128)(2,1)S(1)}, u32[]{:S(2)}) copy-start(bf16[1536,128]{1,0:T(8,128)(2,1)S(1)} %collective-permute-done.7.refs_6_) | copy-start | bytes 1179652
  106.4 0.8 copy-start.12
  112.7 5.9 %collective-permute-start.9 = (f32[8,128,512]{2,1,0:T(8,128)}, f32[8,128,512]{2,1,0:T(8,128)}, u32[]{:S(2)}, u32[]{:S(2)}) collective-permute-start(f32[8,128,512]{2,1,0:T(8,128)} %shard_map.77), channel_id=1, source_target_pairs={{0,16},{16,0},{1,17},{17,1},{2,18},{18,2},{3,19},{19,3},{4,20},{20... | collective-permute-start | bytes 6291464 | tf_op jit(solution)/shard_map/ppermute | solution.py:138
  118.6 6.0 %copy-start.2 = (bf16[1536,512]{1,0:T(8,128)(2,1)S(1)}, bf16[1536,512]{1,0:T(8,128)(2,1)}, u32[]{:S(2)}) copy-start(bf16[1536,512]{1,0:T(8,128)(2,1)} %get-tuple-element.9.refs_8_) | copy-start | bytes 4718596
  132.6 33.0 %collective-permute-start.10 = (f32[8,256,512]{1,2,0:T(8,128)}, f32[8,256,512]{1,2,0:T(8,128)}, u32[]{:S(2)}, u32[]{:S(2)}) collective-permute-start(f32[8,256,512]{1,2,0:T(8,128)} %convolution_bitcast_fusion), channel_id=1, source_target_pairs={{0,16},{16,0},{1,17},{17,1},{2,18},{18,2},{3,19},{19,3},{4,20},{20... | collective-permute-start | bytes 12582920 | tf_op jit(solution)/shard_map/ppermute | solution.py:138
  133.0 40.7 %all-to-all-start.3 = ((bf16[8,128,512]{2,1,0:T(8,128)(2,1)}), bf16[8,128,512]{2,1,0:T(8,128)(2,1)}, u32[]{:S(2)}, u32[]{:S(2)}) async-start(bf16[8,128,512]{2,1,0:T(8,128)(2,1)} %shard_map.78), calls=%async_computation.3 | async-start | bytes 2097152 | tf_op jit(solution)/shard_map/all_to_all | solution.py:132
  159.2 6.4 %copy-start.3 = (bf16[1536,512]{1,0:T(8,128)(2,1)S(1)}, bf16[1536,512]{1,0:T(8,128)(2,1)}, u32[]{:S(2)}) copy-start(bf16[1536,512]{1,0:T(8,128)(2,1)} %get-tuple-element.26.refs_8_) | copy-start | bytes 4718596
  164.3 19.6 %collective-permute-start.13 = (f32[8,128,512]{1,2,0:T(8,128)}, f32[8,128,512]{1,2,0:T(8,128)}, u32[]{:S(2)}, u32[]{:S(2)}) collective-permute-start(f32[8,128,512]{1,2,0:T(8,128)} %convolution_bitcast_fusion.1), channel_id=1, source_target_pairs={{0,16},{16,0},{1,17},{17,1},{2,18},{18,2},{3,19},{19,3},{4,20},{20... | collective-permute-start | bytes 6291464 | tf_op jit(solution)/shard_map/ppermute | solution.py:138
  173.7 6.6 %copy-start.4 = (bf16[1536,512]{1,0:T(8,128)(2,1)S(1)}, bf16[1536,512]{1,0:T(8,128)(2,1)}, u32[]{:S(2)}) copy-start(bf16[1536,512]{1,0:T(8,128)(2,1)} %get-tuple-element.26.refs_8_) | copy-start | bytes 4718596
  173.7 37.9 %all-to-all-start.2 = ((bf16[8,256,512]{1,2,0:T(8,128)(2,1)}), bf16[8,256,512]{1,2,0:T(8,128)(2,1)}, u32[]{:S(2)}, u32[]{:S(2)}) async-start(bf16[8,256,512]{1,2,0:T(8,128)(2,1)} %fusion), calls=%async_computation.2 | async-start | bytes 4194304 | tf_op jit(solution)/shard_map/all_to_all | solution.py:132
  211.6 19.3 %all-to-all-start.4 = ((bf16[8,128,512]{1,2,0:T(8,128)(2,1)}), bf16[8,128,512]{1,2,0:T(8,128)(2,1)S(1)}, u32[]{:S(2)}, u32[]{:S(2)}) async-start(bf16[8,128,512]{1,2,0:T(8,128)(2,1)} %fusion.1), calls=%async_computation.4 | async-start | bytes 2097152 | tf_op jit(solution)/shard_map/all_to_all | solution.py:132
  217.2 30.4 %collective-permute-start.11 = (f32[256,512]{0,1:T(8,128)S(1)}, f32[256,512]{0,1:T(8,128)}, u32[]{:S(2)}, u32[]{:S(2)}) collective-permute-start(f32[256,512]{0,1:T(8,128)S(1)} %convert_reduce_fusion), channel_id=1, source_target_pairs={{0,0},{1,16},{16,1},{17,17},{2,2},{3,18},{18,3},{19,19},{4,4},{5,2... | collective-permute-start | bytes 1572872 | tf_op jit(solution)/shard_map/ppermute | solution.py:134
  223.0 24.7 %collective-permute-start.12 = (f32[128,512]{0,1:T(8,128)}, f32[128,512]{0,1:T(8,128)}, u32[]{:S(2)}, u32[]{:S(2)}) collective-permute-start(f32[128,512]{0,1:T(8,128)} %copy.20), channel_id=1, source_target_pairs={{0,0},{1,16},{16,1},{17,17},{2,2},{3,18},{18,3},{19,19},{4,4},{5,2... | collective-permute-start | bytes 786440 | tf_op jit(solution)/shard_map/ppermute | solution.py:134
  231.0 16.6 %collective-permute-start.14 = (f32[128,512]{0,1:T(8,128)S(1)}, f32[128,512]{0,1:T(8,128)S(1)}, u32[]{:S(2)}, u32[]{:S(2)}) collective-permute-start(f32[128,512]{0,1:T(8,128)S(1)} %convert_reduce_fusion.1), channel_id=1, source_target_pairs={{0,0},{1,16},{16,1},{17,17},{2,2},{3,18},{18,3},{19,19},{4,4},{5,2... | collective-permute-start | bytes 786440 | tf_op jit(solution)/shard_map/ppermute | solution.py:134
  235.0 1.2 collective-permute-start.15
Sparse Core Ops, SparseCore 0:
  9.8 104.3 all-gather.4
  116.0 43.1 all-gather.6

commit v4 on v3

--- a/solution.py
+++ b/solution.py
@@ -25,37 +25,33 @@
     return lax.all_to_all(sent, axis, 0, 0, tiled=True).sum(axis=0)
 
 
-def product(place, blocks, right, added=None):
-    count, (rows, width), cols = len(blocks), blocks[0].shape, right.shape[1]
-    dtype = f32 if added is None else bf16
+def product(place, blocks, right):
+    count, (rows, width), cols = len(blocks) - 1, blocks[0].shape, right.shape[1]
 
     def kernel(place_ref, *refs):
-        right_ref, out_ref = refs[count], refs[-1]
-        for i in range(count):
-            part = lax.dot_general(
-                refs[i][...],
-                right_ref[...],
-                (((0,), (0,)), ((), ())),
-                preferred_element_type=f32,
-            )
-            at = place_ref[i]
-            if added is not None:
-                part = part + refs[count + 1][at]
-            out_ref[at] = part.astype(dtype)
+        right_ref, out_ref = refs[-2:]
+        by_rows = (((0,), (0,)), ((), ()))
 
-    extra = [] if added is None else [added]
+        def part(left_ref, begin):
+            some = right_ref[begin : begin + left_ref.shape[0]]
+            return lax.dot_general(left_ref[...], some, by_rows, preferred_element_type=f32)
+
+        for i in range(count - 1):
+            out_ref[place_ref[i]] = part(refs[i], 0)
+        out_ref[place_ref[count - 1]] = part(refs[count - 1], 0) + part(refs[count], rows // 2)
+
     vmem = pl.BlockSpec(memory_space=pltpu.VMEM)
     return pl.pallas_call(
         kernel,
-        out_shape=jax.ShapeDtypeStruct((count, width, cols), dtype),
-        in_specs=[pl.BlockSpec(memory_space=pltpu.SMEM)] + [vmem] * (count + 1 + len(extra)),
+        out_shape=jax.ShapeDtypeStruct((count, width, cols), f32),
+        in_specs=[pl.BlockSpec(memory_space=pltpu.SMEM)] + [vmem] * (count + 2),
         out_specs=vmem,
         cost_estimate=pl.CostEstimate(
             flops=2 * count * rows * width * cols,
             bytes_accessed=2 * count * rows * width + 2 * rows * cols + 4 * count * width * cols,
             transcendentals=0,
         ),
-    )(place, *blocks, right, *extra)
+    )(place, *blocks, right)
 
 
 def local(design, observations, solution, arc_ids, block_live):
@@ -75,12 +71,17 @@
 
     def hop(ring):
         d = (len(ring["blocks"]) + 1) // 2
-        for side in range(2 if d < n // 2 else 1):
+        half = rows // 2
+        for side in range(2):
             way = up if side == ring["flip"] else down
-            end = lax.ppermute(ring["ends"][side], "z", way)
+            end = ring["ends"][side]
+            if d == n // 2:
+                end = end[side * half : (side + 1) * half]
+            end = lax.ppermute(end, "z", way)
             ring["ends"][side] = end
             ring["blocks"].append(end)
-            ring["steps"].append(-d if way is up else d)
+            if d < n // 2 or side == 0:
+                ring["steps"].append(-d if way is up else d)
         return ring["blocks"][-2:]
 
     def stacked(ring):
@@ -90,7 +91,6 @@
     hops = [hop(early) for _ in range(n // 2)]
     partial_value = jnp.dot(design.astype(f32), solution, precision=lax.Precision.HIGHEST)
     from_pair = lax.ppermute(partial_value, "yl", PAIR)
-    other = lax.ppermute(after(design, from_pair), "yl", PAIR)
     predicted = of_everyone(partial_value + from_pair, "z")
     residual = after(observations - predicted, *hops[0])
     live_row = (
@@ -103,6 +103,7 @@
     arc_squares = jnp.sum(arc_match * squares[None, :], axis=1)
     arc_counts = jnp.sum(arc_match * live_row[None, :], axis=1)
     totals = of_everyone(jnp.stack([jnp.sum(arc_squares), jnp.sum(arc_counts)]), ARCS)
+    other = lax.ppermute(after(design, totals), "yl", PAIR)
     variance_all = (totals[0] + 1.0) / (totals[1] + 1.0)
     arc_weight = variance_all / (
         (arc_squares + prior_rows * variance_all) / (arc_counts + prior_rows)
@@ -124,8 +125,9 @@
 
     def share(left, right, added=None):
         if isinstance(left, tuple):
-            return product(*left, right, added)
-        out = lax.dot_general(left, right, (((1,), (0,)), ((), ())), preferred_element_type=f32)
+            out = product(*left, right)
+        else:
+            out = lax.dot_general(left, right, (((1,), (0,)), ((), ())), preferred_element_type=f32)
         return out if added is None else (out + added).astype(bf16)
 
     def spread(pair):

time: 258 us -> 256 us (level)
  blocking collectives: 10.9 us -> 28.1 us
  waiting for transfers between devices: 106 us -> 96.2 us
  starting transfers between devices: 57.6 us -> 48 us
    all_to_all x1 -> x2, blocking collectives: 10.9 us -> 28.1 us  [of_everyone(): return lax.all_to_all(sent, axis, 0, 0, tiled=True).sum(axis=0)]
    all_to_all x2 -> x1, starting transfers between devices: 16.4 us -> 5.28 us  [of_everyone(): return lax.all_to_all(sent, axis, 0, 0, tiled=True).sum(axis=0)]
    all_to_all x2 -> x1, waiting for transfers between devices: 14.2 us -> 7.57 us  [of_everyone(): return lax.all_to_all(sent, axis, 0, 0, tiled=True).sum(axis=0)]
    ppermute x8 -> x9, waiting for transfers between devices: 32.7 us -> 36.9 us  [the longest x8 36.9 us: hop(): end = lax.ppermute(end, 'z', way)]
    ppermute x3, waiting for transfers between devices: 4.11 us -> 0.01 us  [whole_chunk(): from_core = lax.ppermute(sent, 'core', PAIR)]
    convert_element_type x1 -> x2, other arithmetic: 2.77 us -> 6.56 us  [share(): return out if added is None else (out + added).astype(bf16)]
    all_gather x1, waiting for transfers between devices: 21.9 us -> 18.4 us  [local(): last = lax.all_gather(design[:, FIRST + WIDTH:], 'z', axis=0)]
    ppermute x8 -> x9, starting transfers between devices: 13.1 us -> 14.9 us  [the longest x8 14.6 us: hop(): end = lax.ppermute(end, 'z', way)]
  transfers between devices with their start and end apart: 23 -> 23, of which waited for: 10 -> 9; matrix products, arithmetic and copies ran while one was open for 19% -> 19% of each run, Pallas kernels for 5% -> 4%
where the time goes in v4:
time: 256 us; the launch traced here: 255 us
  waiting for transfers between devices  96.2 us (38%)
  starting transfers between devices  48 us (19%)
  blocking collectives  28.1 us (11%)
  matrix products  27.2 us (11%)
  other arithmetic  19.9 us (8%)
  between operations  15.7 us (6%)
  Pallas kernels  11.1 us (4%)
  local copies, waits for them, and re-layouts  8.81 us (3%)
    ppermute x8, waiting for transfers between devices, hop(): end = lax.ppermute(end, 'z', way)  36.9 us
    all_to_all x3, waiting for transfers between devices, spread(): got = lax.all_to_all(pair, ('x', 'yh'), 0, 0, tiled=True)  30.6 us
    all_to_all x2, blocking collectives, of_everyone(): return lax.all_to_all(sent, axis, 0, 0, tiled=True).sum(axis=0)  28.1 us
    dot_general x4, matrix products, share(): lax.dot_general(left, right, (((1,), (0,)), ((), ())), preferred_element_...  25.2 us
    all_gather x1, waiting for transfers between devices, local(): last = lax.all_gather(design[:, FIRST + WIDTH:], 'z', axis=0)  18.4 us
    ppermute x8, starting transfers between devices, hop(): end = lax.ppermute(end, 'z', way)  14.6 us
    all_to_all x3, starting transfers between devices, spread(): got = lax.all_to_all(pair, ('x', 'yh'), 0, 0, tiled=True)  14.4 us
    pallas_call x2, Pallas kernels, product(): pl.pallas_call(kernel, out_shape=jax.ShapeDtypeStruct((count, width, cols...  11.1 us
  transfers between devices with their start and end apart: 23, of which 9 were waited for; matrix products, arithmetic and copies ran while one was open for 19% of the time, Pallas kernels for 4%

profile of v4, /device:TPU:1, one launch (start us, length us, event | category | flops | bytes accessed | tf_op | source)
XLA Modules:
  0.0 255.1 jit_solution(16622093730192955797)
XLA Ops:
  7.2 0.0 all-gather.5.cloned.1.call-start
  7.2 2.2 slice.24
  9.5 0.8 fusion.9
  10.3 2.5 collective-permute-start.1
  12.8 3.9 %collective-permute-start.2 = (bf16[1536,128]{1,0:T(8,128)(2,1)S(1)}, bf16[1536,128]{1,0:T(8,128)(2,1)S(1)}, u32[]{:S(2)}, u32[]{:S(2)}) collective-permute-start(bf16[1536,128]{1,0:T(8,128)(2,1)S(1)} %get-tuple-element.28.refs_0_), channel_id=1, source_target_pairs={{0,14},{2,0},{4,2},{6,4},{8,6},{10,8},{12,10},{14,12},{1,15},{3,1}... | collective-permute-start | bytes 1179656 | tf_op jit(solution)/shard_map/ppermute | solution.py:80
  16.7 1.3 convolution_reduce_fusion
  18.1 1.4 collective-permute-start
  19.5 1.5 collective-permute-done
  21.0 0.6 broadcast_in_dim.9
  21.6 5.3 %all-to-all-start = ((f32[8,1,1536]{2,1,0:T(1,128)}), f32[8,1,1536]{2,1,0:T(1,128)S(1)}, u32[]{:S(2)}, u32[]{:S(2)}) async-start(f32[8,1,1536]{2,1,0:T(1,128)} %broadcast_in_dim.9), calls=%async_computation | async-start | bytes 98304 | tf_op jit(solution)/shard_map/all_to_all | solution.py:25
  26.9 0.0 all-gather.7.cloned.1.call-start
  26.9 0.1 broadcast_bitcast_fusion
  27.0 7.6 %all-to-all-done = f32[8,1,1536]{2,1,0:T(1,128)S(1)} async-done(((f32[8,1,1536]{2,1,0:T(1,128)}), f32[8,1,1536]{2,1,0:T(1,128)S(1)}, u32[]{:S(2)}, u32[]{:S(2)}) %all-to-all-start) | async-done | bytes 49184 | tf_op jit(solution)/shard_map/all_to_all | solution.py:25
  34.7 0.1 multiply_multiply_fusion
  34.8 0.8 select_reduce_fusion.3
  35.6 1.4 pad_maximum_fusion.1
  37.0 17.3 %all_to_all.33 = f32[16,1,2]{2,1,0:T(1,128)S(1)} all-to-all(f32[16,1,2]{2,1,0:T(1,128)S(1)} %broadcast_in_dim.10), channel_id=1, replica_groups=mesh['x'=4,'yh'=2,'core'=2,'z'=8,'yl'=2] {'x','yh','core'}, dimensions={0} | all-to-all | bytes 256 | tf_op jit(solution)/shard_map/all_to_all | solution.py:25
  54.2 0.5 reduce_sum.102
  54.8 0.4 collective-permute-start.5
  55.2 0.3 collective-permute-start.3
  55.5 2.4 collective-permute-start.4
  57.9 1.2 compare_select_fusion.place_ref
  59.1 1.4 fusion.10
  61.9 14.0 %collective-permute-done.3.refs_3_ = bf16[1536,128]{1,0:T(8,128)(2,1)} collective-permute-done((bf16[1536,128]{1,0:T(8,128)(2,1)}, bf16[1536,128]{1,0:T(8,128)(2,1)}, u32[]{:S(2)}, u32[]{:S(2)}) %collective-permute-start.3) | collective-permute-done | bytes 393248 | tf_op jit(solution)/shard_map/ppermute | solution.py:80
  76.0 2.7 %collective-permute-start.7 = (bf16[1536,128]{1,0:T(8,128)(2,1)}, bf16[1536,128]{1,0:T(8,128)(2,1)S(1)}, u32[]{:S(2)}, u32[]{:S(2)}) collective-permute-start(bf16[1536,128]{1,0:T(8,128)(2,1)} %collective-permute-done.4.refs_4_), channel_id=1, source_target_pairs={{0,14},{2,0},{4,2},{6,4},{8,6},{10,8},{12,10},{14,12},{1,15},{3,1}... | collective-permute-start | bytes 1179656 | tf_op jit(solution)/shard_map/ppermute | solution.py:80
  78.6 0.7 add_divide_fusion
  79.3 0.1 select_reduce_fusion.4
  79.4 0.8 fusion.8
  80.2 16.3 %collective-permute-done.6.refs_5_ = bf16[1536,128]{1,0:T(8,128)(2,1)S(1)} collective-permute-done((bf16[1536,128]{1,0:T(8,128)(2,1)}, bf16[1536,128]{1,0:T(8,128)(2,1)S(1)}, u32[]{:S(2)}, u32[]{:S(2)}) %collective-permute-start.6) | collective-permute-done | bytes 393248 | tf_op jit(solution)/shard_map/ppermute | solution.py:80
  96.5 0.1 collective-permute-start.8
  96.7 2.7 %collective-permute-start.9 = (bf16[768,128]{1,0:T(8,128)(2,1)S(1)}, bf16[768,128]{1,0:T(8,128)(2,1)S(1)}, u32[]{:S(2)}, u32[]{:S(2)}) collective-permute-start(bf16[768,128]{1,0:T(8,128)(2,1)S(1)} %slice.29), channel_id=1, source_target_pairs={{0,14},{2,0},{4,2},{6,4},{8,6},{10,8},{12,10},{14,12},{1,15},{3,1}... | collective-permute-start | bytes 589832 | tf_op jit(solution)/shard_map/ppermute | solution.py:80
  99.4 2.4 broadcast_select_fusion.1
  101.8 6.5 %collective-permute-done.8.refs_7_ = bf16[768,128]{1,0:T(8,128)(2,1)S(1)} collective-permute-done((bf16[768,128]{1,0:T(8,128)(2,1)S(1)}, bf16[768,128]{1,0:T(8,128)(2,1)S(1)}, u32[]{:S(2)}, u32[]{:S(2)}) %collective-permute-start.8) | collective-permute-done | bytes 196640 | tf_op jit(solution)/shard_map/ppermute | solution.py:80
  108.3 0.7 copy-done.9
  109.0 0.7 copy-done.10
  109.7 5.5 %shard_map.78 = f32[8,128,512]{2,1,0:T(8,128)} custom-call(s32[8]{0:T(128)} %compare_select_fusion.place_ref, bf16[1536,128]{1,0:T(8,128)(2,1)} %copy-done.4, bf16[1536,128]{1,0:T(8,128)(2,1)} %copy-done.7, bf16[1536,128]{1,0:T(8,128)(2,1)} %copy-done.8, bf16[1536,128]{1,0:T(8,128)(2,1)} %collective-permute-done.3.refs_3_, ...), custom_call_target="tpu_custom_call" | custom-call | flops 1610612736 | bytes 6815744 | tf_op jit(solution)/shard_map/pallas_call | solution.py:44
  115.2 1.9 collective-permute-start.10
  117.2 5.5 %shard_map.77 = f32[8,128,512]{2,1,0:T(8,128)} custom-call(s32[8]{0:T(128)} %compare_select_fusion.place_ref, bf16[1536,128]{1,0:T(8,128)(2,1)} %copy-done.4, bf16[1536,128]{1,0:T(8,128)(2,1)} %copy-done.7, bf16[1536,128]{1,0:T(8,128)(2,1)} %copy-done.8, bf16[1536,128]{1,0:T(8,128)(2,1)} %collective-permute-done.3.refs_3_, ...), custom_call_target="tpu_custom_call" | custom-call | flops 1610612736 | bytes 6815744 | tf_op jit(solution)/shard_map/pallas_call | solution.py:44
  122.7 3.8 %add_convert_fusion = bf16[8,128,512]{2,1,0:T(8,128)(2,1)} fusion(f32[8,128,512]{2,1,0:T(8,128)} %shard_map.77, f32[8,128,512]{2,1,0:T(8,128)} %collective-permute-done.10), kind=kLoop, calls=%fused_computation.10 | loop fusion | flops 1048576 | bytes 5242880 | tf_op jit(solution)/shard_map/convert_element_type | solution.py:131
  126.5 7.8 %convolution_bitcast_fusion = f32[8,256,512]{1,2,0:T(8,128)} fusion(bf16[8,1536,256]{2,1,0:T(8,128)(2,1)} %bitcast.48, bf16[1536,512]{1,0:T(8,128)(2,1)S(1)} %copy-done.3), kind=kOutput, calls=%fused_computation.5 | convolution fusion | flops 3221225472 | bytes 12058624 | tf_op jit(solution)/shard_map/dot_general | solution.py:130
  134.3 4.2 %all-to-all-start.3 = ((bf16[8,128,512]{2,1,0:T(8,128)(2,1)}), bf16[8,128,512]{2,1,0:T(8,128)(2,1)}, u32[]{:S(2)}, u32[]{:S(2)}) async-start(bf16[8,128,512]{2,1,0:T(8,128)(2,1)} %add_convert_fusion), calls=%async_computation.3 | async-start | bytes 2097152 | tf_op jit(solution)/shard_map/all_to_all | solution.py:134
  138.5 18.4 %all-gather.7.cloned.1.call-done = bf16[12288,128]{1,0:T(8,128)(2,1)} async-done(((bf16[1536,128]{1,0:T(8,128)(2,1)}), bf16[12288,128]{1,0:T(8,128)(2,1)}) %all-gather.7.cloned.1.call-update) | async-done | bytes 3145744 | tf_op jit(solution)/shard_map/all_gather | solution.py:65
  157.0 5.6 %convolution_bitcast_fusion.1 = f32[8,128,512]{1,2,0:T(8,128)} fusion(bf16[8,1536,128]{2,1,0:T(8,128)(2,1)} %bitcast.50, bf16[1536,512]{1,0:T(8,128)(2,1)} %get-tuple-element.9.refs_9_), kind=kOutput, calls=%fused_computation.11 | convolution fusion | flops 1610612736 | bytes 6815744 | tf_op jit(solution)/shard_map/dot_general | solution.py:130
  162.6 1.2 collective-permute-start.14
  163.8 8.1 %fusion = bf16[8,256,512]{1,2,0:T(8,128)(2,1)} fusion(f32[8,256,512]{1,2,0:T(8,128)} %collective-permute-done.11, bf16[8,1536,256]{2,1,0:T(8,128)(2,1)} %bitcast.49, bf16[1536,512]{1,0:T(8,128)(2,1)S(1)} %copy-done.2), kind=kOutput, calls=%fused_computation.1 | convolution fusion | flops 3223322624 | bytes 14155776 | tf_op jit(solution)/shard_map/dot_general | solution.py:130
  171.9 6.5 %all-to-all-start.2 = ((bf16[8,256,512]{1,2,0:T(8,128)(2,1)}), bf16[8,256,512]{1,2,0:T(8,128)(2,1)}, u32[]{:S(2)}, u32[]{:S(2)}) async-start(bf16[8,256,512]{1,2,0:T(8,128)(2,1)} %fusion), calls=%async_computation.2 | async-start | bytes 4194304 | tf_op jit(solution)/shard_map/all_to_all | solution.py:134
  178.3 3.7 %fusion.4 = f32[512,8,128]{2,0,1:T(8,128)S(1)} fusion(bf16[8,1536,128]{2,1,0:T(8,128)(2,1)} %bitcast.51, bf16[1536,512]{1,0:T(8,128)(2,1)S(1)} %copy-done.2), kind=kOutput, calls=%fused_computation.14 | convolution fusion | flops 1610612736 | bytes 6815744 | tf_op jit(solution)/shard_map/dot_general | solution.py:130
  182.1 2.8 %fusion.1 = bf16[8,128,512]{1,2,0:T(8,128)(2,1)} fusion(f32[8,128,512]{1,2,0:T(8,128)} %collective-permute-done.14, f32[512,8,128]{2,0,1:T(8,128)S(1)} %fusion.4), kind=kLoop, calls=%fused_computation.7 | loop fusion | flops 1048576 | bytes 5242880 | tf_op jit(solution)/shard_map/convert_element_type | solution.py:131
  184.9 24.8 %all-to-all-done.2 = bf16[8,256,512]{1,2,0:T(8,128)(2,1)} async-done(((bf16[8,256,512]{1,2,0:T(8,128)(2,1)}), bf16[8,256,512]{1,2,0:T(8,128)(2,1)}, u32[]{:S(2)}, u32[]{:S(2)}) %all-to-all-start.2) | async-done | bytes 2097184 | tf_op jit(solution)/shard_map/all_to_all | solution.py:134
  209.7 3.7 %all-to-all-start.4 = ((bf16[8,128,512]{1,2,0:T(8,128)(2,1)}), bf16[8,128,512]{1,2,0:T(8,128)(2,1)S(1)}, u32[]{:S(2)}, u32[]{:S(2)}) async-start(bf16[8,128,512]{1,2,0:T(8,128)(2,1)} %fusion.1), calls=%async_computation.4 | async-start | bytes 2097152 | tf_op jit(solution)/shard_map/all_to_all | solution.py:134
  213.4 1.9 convert_reduce_fusion
  215.3 3.5 %collective-permute-start.12 = (f32[256,512]{0,1:T(8,128)S(1)}, f32[256,512]{0,1:T(8,128)}, u32[]{:S(2)}, u32[]{:S(2)}) collective-permute-start(f32[256,512]{0,1:T(8,128)S(1)} %convert_reduce_fusion), channel_id=1, source_target_pairs={{0,0},{1,16},{16,1},{17,17},{2,2},{3,18},{18,3},{19,19},{4,4},{5,2... | collective-permute-start | bytes 1572872 | tf_op jit(solution)/shard_map/ppermute | solution.py:136
  218.8 1.4 convert_reduce_fusion.2
  220.2 0.8 copy.20
  221.0 2.1 collective-permute-start.13
  223.1 5.8 %all-to-all-done.4 = bf16[8,128,512]{1,2,0:T(8,128)(2,1)S(1)} async-done(((bf16[8,128,512]{1,2,0:T(8,128)(2,1)}), bf16[8,128,512]{1,2,0:T(8,128)(2,1)S(1)}, u32[]{:S(2)}, u32[]{:S(2)}) %all-to-all-start.4) | async-done | bytes 1048608 | tf_op jit(solution)/shard_map/all_to_all | solution.py:134
  228.9 0.1 convert_reduce_fusion.1
  229.1 3.2 %collective-permute-start.15 = (f32[128,512]{0,1:T(8,128)S(1)}, f32[128,512]{0,1:T(8,128)S(1)}, u32[]{:S(2)}, u32[]{:S(2)}) collective-permute-start(f32[128,512]{0,1:T(8,128)S(1)} %convert_reduce_fusion.1), channel_id=1, source_target_pairs={{0,0},{1,16},{16,1},{17,17},{2,2},{3,18},{18,3},{19,19},{4,4},{5,2... | collective-permute-start | bytes 786440 | tf_op jit(solution)/shard_map/ppermute | solution.py:136
  232.3 0.7 fusion.11
  233.1 1.2 collective-permute-done.16
  234.2 10.9 %all_to_all.34 = f32[8,1,512]{2,1,0:T(1,128)S(1)} all-to-all(f32[8,1,512]{2,1,0:T(1,128)S(1)} %broadcast_in_dim.11), channel_id=1, replica_groups=mesh['x'=4,'yh'=2,'core'=2,'z'=8,'yl'=2] {'x','yh'}, dimensions={0} | all-to-all | bytes 32768 | tf_op jit(solution)/shard_map/all_to_all | solution.py:25
  245.1 0.6 reduce_sum.109
  245.7 1.2 pad_maximum_fusion
  246.9 1.3 copy.22
  (58 shorter events, 0.3 us)
Async XLA Ops:
  7.2 9.6 %copy-start = (f32[512]{0:T(512)S(1)}, f32[512]{0:T(512)}, u32[]{:S(2)}) copy-start(f32[512]{0:T(512)} %param.8) | copy-start | bytes 6148
  7.2 2.3 copy-start.1
  7.2 119.3 %all-gather.5.cloned.1.call-start = ((), (), s32[]{:S(2)}) async-start(), calls=%async_computation.6 | async-start | bytes 7077888 | tf_op jit(solution)/shard_map/all_gather | solution.py:64
  9.5 10.0 %copy-start.14 = (s32[1,12]{1,0:T(1,128)S(1)}, s32[1,12]{1,0:T(1,128)}, u32[]{:S(2)}) copy-start(s32[1,12]{1,0:T(1,128)} %param.10) | copy-start | bytes 148
  9.5 17.5 %copy-start.13 = (s32[1,1536]{1,0:T(1,128)S(1)}, s32[1,1536]{1,0:T(1,128)}, u32[]{:S(2)}) copy-start(s32[1,1536]{1,0:T(1,128)} %param.9) | copy-start | bytes 18436
  9.5 25.2 %copy-start.12 = (f32[1536]{0:T(1024)S(1)}, f32[1536]{0:T(1024)}, u32[]{:S(2)}) copy-start(f32[1536]{0:T(1024)} %param.7) | copy-start | bytes 18436
  10.3 91.5 %copy-start.4 = (bf16[1536,128]{1,0:T(8,128)(2,1)}, bf16[1536,128]{1,0:T(8,128)(2,1)S(1)}, u32[]{:S(2)}) copy-start(bf16[1536,128]{1,0:T(8,128)(2,1)S(1)} %get-tuple-element.28.refs_0_) | copy-start | bytes 1179652
  10.3 24.3 %collective-permute-start.1 = (bf16[1536,128]{1,0:T(8,128)(2,1)S(1)}, bf16[1536,128]{1,0:T(8,128)(2,1)S(1)}, u32[]{:S(2)}, u32[]{:S(2)}) collective-permute-start(bf16[1536,128]{1,0:T(8,128)(2,1)S(1)} %get-tuple-element.28.refs_0_), channel_id=1, source_target_pairs={{0,2},{2,4},{4,6},{6,8},{8,10},{10,12},{12,14},{14,0},{1,3},{3,5},... | collective-permute-start | bytes 1179656 | tf_op jit(solution)/shard_map/ppermute | solution.py:80
  12.8 21.9 %collective-permute-start.2 = (bf16[1536,128]{1,0:T(8,128)(2,1)S(1)}, bf16[1536,128]{1,0:T(8,128)(2,1)S(1)}, u32[]{:S(2)}, u32[]{:S(2)}) collective-permute-start(bf16[1536,128]{1,0:T(8,128)(2,1)S(1)} %get-tuple-element.28.refs_0_), channel_id=1, source_target_pairs={{0,14},{2,0},{4,2},{6,4},{8,6},{10,8},{12,10},{14,12},{1,15},{3,1}... | collective-permute-start | bytes 1179656 | tf_op jit(solution)/shard_map/ppermute | solution.py:80
  18.1 2.9 %collective-permute-start = (f32[1536]{0:T(1024)S(1)}, f32[1536]{0:T(1024)S(1)}, u32[]{:S(2)}, u32[]{:S(2)}) collective-permute-start(f32[1536]{0:T(1024)S(1)} %convolution_reduce_fusion), channel_id=1, source_target_pairs={{0,1},{1,0},{2,3},{3,2},{4,5},{5,4},{6,7},{7,6},{8,9},{9,8},{10,11... | collective-permute-start | bytes 18440 | tf_op jit(solution)/shard_map/ppermute | solution.py:93
  21.6 13.0 %all-to-all-start = ((f32[8,1,1536]{2,1,0:T(1,128)}), f32[8,1,1536]{2,1,0:T(1,128)S(1)}, u32[]{:S(2)}, u32[]{:S(2)}) async-start(f32[8,1,1536]{2,1,0:T(1,128)} %broadcast_in_dim.9), calls=%async_computation | async-start | bytes 98304 | tf_op jit(solution)/shard_map/all_to_all | solution.py:25
  26.9 130.1 %all-gather.7.cloned.1.call-start = ((), (), s32[]{:S(2)}) async-start(), calls=%async_computation.7 | async-start | bytes 3538944 | tf_op jit(solution)/shard_map/all_gather | solution.py:65
  34.7 19.6 %copy-start.11 = (f32[1536]{0:T(1024)}, f32[1536]{0:T(1024)S(1)}, u32[]{:S(2)}) copy-start(f32[1536]{0:T(1024)S(1)} %sub.3) | copy-start | bytes 18436
  34.7 19.5 %copy-start.7 = (bf16[1536,128]{1,0:T(8,128)(2,1)}, bf16[1536,128]{1,0:T(8,128)(2,1)S(1)}, u32[]{:S(2)}) copy-start(bf16[1536,128]{1,0:T(8,128)(2,1)S(1)} %collective-permute-done.1.refs_1_) | copy-start | bytes 1179652
  34.7 19.5 %copy-start.8 = (bf16[1536,128]{1,0:T(8,128)(2,1)}, bf16[1536,128]{1,0:T(8,128)(2,1)S(1)}, u32[]{:S(2)}) copy-start(bf16[1536,128]{1,0:T(8,128)(2,1)S(1)} %collective-permute-done.2.refs_2_) | copy-start | bytes 1179652
  54.8 44.6 %collective-permute-start.5 = (bf16[1536,512]{1,0:T(8,128)(2,1)S(1)}, bf16[1536,512]{1,0:T(8,128)(2,1)S(1)}, u32[]{:S(2)}, u32[]{:S(2)}) collective-permute-start(bf16[1536,512]{1,0:T(8,128)(2,1)S(1)} %copy-done.1), channel_id=1, source_target_pairs={{0,1},{1,0},{2,3},{3,2},{4,5},{5,4},{6,7},{7,6},{8,9},{9,8},{10,11... | collective-permute-start | bytes 4718600 | tf_op jit(solution)/shard_map/ppermute | solution.py:106
  55.2 20.8 %collective-permute-start.3 = (bf16[1536,128]{1,0:T(8,128)(2,1)}, bf16[1536,128]{1,0:T(8,128)(2,1)}, u32[]{:S(2)}, u32[]{:S(2)}) collective-permute-start(bf16[1536,128]{1,0:T(8,128)(2,1)} %copy-done.7), channel_id=1, source_target_pairs={{0,2},{2,4},{4,6},{6,8},{8,10},{10,12},{12,14},{14,0},{1,3},{3,5},... | collective-permute-start | bytes 1179656 | tf_op jit(solution)/shard_map/ppermute | solution.py:80
  55.5 20.5 %collective-permute-start.4 = (bf16[1536,128]{1,0:T(8,128)(2,1)}, bf16[1536,128]{1,0:T(8,128)(2,1)}, u32[]{:S(2)}, u32[]{:S(2)}) collective-permute-start(bf16[1536,128]{1,0:T(8,128)(2,1)} %copy-done.8), channel_id=1, source_target_pairs={{0,14},{2,0},{4,2},{6,4},{8,6},{10,8},{12,10},{14,12},{1,15},{3,1}... | collective-permute-start | bytes 1179656 | tf_op jit(solution)/shard_map/ppermute | solution.py:80
  76.0 20.5 %collective-permute-start.6 = (bf16[1536,128]{1,0:T(8,128)(2,1)}, bf16[1536,128]{1,0:T(8,128)(2,1)S(1)}, u32[]{:S(2)}, u32[]{:S(2)}) collective-permute-start(bf16[1536,128]{1,0:T(8,128)(2,1)} %collective-permute-done.3.refs_3_), channel_id=1, source_target_pairs={{0,2},{2,4},{4,6},{6,8},{8,10},{10,12},{12,14},{14,0},{1,3},{3,5},... | collective-permute-start | bytes 1179656 | tf_op jit(solution)/shard_map/ppermute | solution.py:80
  76.0 20.7 %collective-permute-start.7 = (bf16[1536,128]{1,0:T(8,128)(2,1)}, bf16[1536,128]{1,0:T(8,128)(2,1)S(1)}, u32[]{:S(2)}, u32[]{:S(2)}) collective-permute-start(bf16[1536,128]{1,0:T(8,128)(2,1)} %collective-permute-done.4.refs_4_), channel_id=1, source_target_pairs={{0,14},{2,0},{4,2},{6,4},{8,6},{10,8},{12,10},{14,12},{1,15},{3,1}... | collective-permute-start | bytes 1179656 | tf_op jit(solution)/shard_map/ppermute | solution.py:80
  96.5 5.3 %copy-start.5 = (bf16[1536,128]{1,0:T(8,128)(2,1)}, bf16[1536,128]{1,0:T(8,128)(2,1)S(1)}, u32[]{:S(2)}) copy-start(bf16[1536,128]{1,0:T(8,128)(2,1)S(1)} %collective-permute-done.6.refs_5_) | copy-start | bytes 1179652
  96.5 11.8 %collective-permute-start.8 = (bf16[768,128]{1,0:T(8,128)(2,1)S(1)}, bf16[768,128]{1,0:T(8,128)(2,1)S(1)}, u32[]{:S(2)}, u32[]{:S(2)}) collective-permute-start(bf16[768,128]{1,0:T(8,128)(2,1)S(1)} %slice.28), channel_id=1, source_target_pairs={{0,2},{2,4},{4,6},{6,8},{8,10},{10,12},{12,14},{14,0},{1,3},{3,5},... | collective-permute-start | bytes 589832 | tf_op jit(solution)/shard_map/ppermute | solution.py:80
  96.6 5.2 %copy-start.6 = (bf16[1536,128]{1,0:T(8,128)(2,1)}, bf16[1536,128]{1,0:T(8,128)(2,1)S(1)}, u32[]{:S(2)}) copy-start(bf16[1536,128]{1,0:T(8,128)(2,1)S(1)} %collective-permute-done.7.refs_6_) | copy-start | bytes 1179652
  96.7 12.3 %collective-permute-start.9 = (bf16[768,128]{1,0:T(8,128)(2,1)S(1)}, bf16[768,128]{1,0:T(8,128)(2,1)S(1)}, u32[]{:S(2)}, u32[]{:S(2)}) collective-permute-start(bf16[768,128]{1,0:T(8,128)(2,1)S(1)} %slice.29), channel_id=1, source_target_pairs={{0,14},{2,0},{4,2},{6,4},{8,6},{10,8},{12,10},{14,12},{1,15},{3,1}... | collective-permute-start | bytes 589832 | tf_op jit(solution)/shard_map/ppermute | solution.py:80
  108.3 0.7 copy-start.9
  109.0 0.7 copy-start.10
  115.2 7.5 %collective-permute-start.10 = (f32[8,128,512]{2,1,0:T(8,128)}, f32[8,128,512]{2,1,0:T(8,128)}, u32[]{:S(2)}, u32[]{:S(2)}) collective-permute-start(f32[8,128,512]{2,1,0:T(8,128)} %shard_map.78), channel_id=1, source_target_pairs={{0,16},{16,0},{1,17},{17,1},{2,18},{18,2},{3,19},{19,3},{4,20},{20... | collective-permute-start | bytes 6291464 | tf_op jit(solution)/shard_map/ppermute | solution.py:140
  122.7 3.8 %copy-start.3 = (bf16[1536,512]{1,0:T(8,128)(2,1)S(1)}, bf16[1536,512]{1,0:T(8,128)(2,1)}, u32[]{:S(2)}) copy-start(bf16[1536,512]{1,0:T(8,128)(2,1)} %get-tuple-element.9.refs_9_) | copy-start | bytes 4718596
  134.3 29.5 %collective-permute-start.11 = (f32[8,256,512]{1,2,0:T(8,128)}, f32[8,256,512]{1,2,0:T(8,128)}, u32[]{:S(2)}, u32[]{:S(2)}) collective-permute-start(f32[8,256,512]{1,2,0:T(8,128)} %convolution_bitcast_fusion), channel_id=1, source_target_pairs={{0,16},{16,0},{1,17},{17,1},{2,18},{18,2},{3,19},{19,3},{4,20},{20... | collective-permute-start | bytes 12582920 | tf_op jit(solution)/shard_map/ppermute | solution.py:140
  134.3 37.6 %all-to-all-start.3 = ((bf16[8,128,512]{2,1,0:T(8,128)(2,1)}), bf16[8,128,512]{2,1,0:T(8,128)(2,1)}, u32[]{:S(2)}, u32[]{:S(2)}) async-start(bf16[8,128,512]{2,1,0:T(8,128)(2,1)} %add_convert_fusion), calls=%async_computation.3 | async-start | bytes 2097152 | tf_op jit(solution)/shard_map/all_to_all | solution.py:134
  157.0 6.8 %copy-start.2 = (bf16[1536,512]{1,0:T(8,128)(2,1)S(1)}, bf16[1536,512]{1,0:T(8,128)(2,1)}, u32[]{:S(2)}) copy-start(bf16[1536,512]{1,0:T(8,128)(2,1)} %get-tuple-element.26.refs_9_) | copy-start | bytes 4718596
  162.6 19.5 %collective-permute-start.14 = (f32[8,128,512]{1,2,0:T(8,128)}, f32[8,128,512]{1,2,0:T(8,128)}, u32[]{:S(2)}, u32[]{:S(2)}) collective-permute-start(f32[8,128,512]{1,2,0:T(8,128)} %convolution_bitcast_fusion.1), channel_id=1, source_target_pairs={{0,16},{16,0},{1,17},{17,1},{2,18},{18,2},{3,19},{19,3},{4,20},{20... | collective-permute-start | bytes 6291464 | tf_op jit(solution)/shard_map/ppermute | solution.py:140
  171.9 37.8 %all-to-all-start.2 = ((bf16[8,256,512]{1,2,0:T(8,128)(2,1)}), bf16[8,256,512]{1,2,0:T(8,128)(2,1)}, u32[]{:S(2)}, u32[]{:S(2)}) async-start(bf16[8,256,512]{1,2,0:T(8,128)(2,1)} %fusion), calls=%async_computation.2 | async-start | bytes 4194304 | tf_op jit(solution)/shard_map/all_to_all | solution.py:134
  209.7 19.3 %all-to-all-start.4 = ((bf16[8,128,512]{1,2,0:T(8,128)(2,1)}), bf16[8,128,512]{1,2,0:T(8,128)(2,1)S(1)}, u32[]{:S(2)}, u32[]{:S(2)}) async-start(bf16[8,128,512]{1,2,0:T(8,128)(2,1)} %fusion.1), calls=%async_computation.4 | async-start | bytes 2097152 | tf_op jit(solution)/shard_map/all_to_all | solution.py:134
  215.3 30.4 %collective-permute-start.12 = (f32[256,512]{0,1:T(8,128)S(1)}, f32[256,512]{0,1:T(8,128)}, u32[]{:S(2)}, u32[]{:S(2)}) collective-permute-start(f32[256,512]{0,1:T(8,128)S(1)} %convert_reduce_fusion), channel_id=1, source_target_pairs={{0,0},{1,16},{16,1},{17,17},{2,2},{3,18},{18,3},{19,19},{4,4},{5,2... | collective-permute-start | bytes 1572872 | tf_op jit(solution)/shard_map/ppermute | solution.py:136
  221.0 24.7 %collective-permute-start.13 = (f32[128,512]{0,1:T(8,128)}, f32[128,512]{0,1:T(8,128)}, u32[]{:S(2)}, u32[]{:S(2)}) collective-permute-start(f32[128,512]{0,1:T(8,128)} %copy.20), channel_id=1, source_target_pairs={{0,0},{1,16},{16,1},{17,17},{2,2},{3,18},{18,3},{19,19},{4,4},{5,2... | collective-permute-start | bytes 786440 | tf_op jit(solution)/shard_map/ppermute | solution.py:136
  229.1 16.6 %collective-permute-start.15 = (f32[128,512]{0,1:T(8,128)S(1)}, f32[128,512]{0,1:T(8,128)S(1)}, u32[]{:S(2)}, u32[]{:S(2)}) collective-permute-start(f32[128,512]{0,1:T(8,128)S(1)} %convert_reduce_fusion.1), channel_id=1, source_target_pairs={{0,0},{1,16},{16,1},{17,17},{2,2},{3,18},{18,3},{19,19},{4,4},{5,2... | collective-permute-start | bytes 786440 | tf_op jit(solution)/shard_map/ppermute | solution.py:136
  233.1 1.2 collective-permute-start.16
Sparse Core Ops, SparseCore 0:
  9.8 99.4 all-gather.4
  117.3 39.6 all-gather.6

commit v5 on v4

--- a/solution.py
+++ b/solution.py
@@ -2,6 +2,7 @@
 import jax.numpy as jnp
 from jax import lax
 from jax.experimental import pallas as pl
+from jax.experimental.layout import Layout, with_layout_constraint
 from jax.experimental.pallas import tpu as pltpu
 from jax.sharding import Mesh
 from jax.sharding import PartitionSpec as P
@@ -128,11 +129,14 @@
             out = product(*left, right)
         else:
             out = lax.dot_general(left, right, (((1,), (0,)), ((), ())), preferred_element_type=f32)
-        return out if added is None else (out + added).astype(bf16)
+        if added is None:
+            return out
+        return (lax.optimization_barrier(out) + added).astype(bf16)
 
     def spread(pair):
         got = lax.all_to_all(pair, ("x", "yh"), 0, 0, tiled=True)
         block = jnp.sum(got.astype(f32), axis=0)
+        block = with_layout_constraint(block, Layout((0, 1)))
         return lax.ppermute(block, ("core", "yl"), [(0, 0), (1, 2), (2, 1), (3, 3)])
 
     def whole_chunk(left, *tied):

time: 256 us -> 257 us (level)
  other arithmetic: 19.9 us -> 25.8 us
    convert_element_type x2 -> x3, other arithmetic: 6.56 us -> 10.6 us  [share(): return (lax.optimization_barrier(out) + added).astype(bf16)]
  transfers between devices with their start and end apart: 23 -> 23, of which waited for: 9 -> 9; matrix products, arithmetic and copies ran while one was open for 19% -> 20% of each run, Pallas kernels for 4% -> 4%
where the time goes in v5:
time: 257 us; the launch traced here: 256 us
  waiting for transfers between devices  94.6 us (37%)
  starting transfers between devices  48.8 us (19%)
  blocking collectives  28.1 us (11%)
  other arithmetic  25.8 us (10%)
  matrix products  24.8 us (10%)
  between operations  15.7 us (6%)
  Pallas kernels  11.1 us (4%)
  local copies, waits for them, and re-layouts  6.96 us (3%)
    ppermute x8, waiting for transfers between devices, hop(): end = lax.ppermute(end, 'z', way)  36.6 us
    all_to_all x3, waiting for transfers between devices, spread(): got = lax.all_to_all(pair, ('x', 'yh'), 0, 0, tiled=True)  29.8 us
    all_to_all x2, blocking collectives, of_everyone(): return lax.all_to_all(sent, axis, 0, 0, tiled=True).sum(axis=0)  28.1 us
    dot_general x4, matrix products, share(): lax.dot_general(left, right, (((1,), (0,)), ((), ())), preferred_element_...  22.7 us
    all_gather x1, waiting for transfers between devices, local(): last = lax.all_gather(design[:, FIRST + WIDTH:], 'z', axis=0)  17.9 us
    ppermute x8, starting transfers between devices, hop(): end = lax.ppermute(end, 'z', way)  14.6 us
    all_to_all x3, starting transfers between devices, spread(): got = lax.all_to_all(pair, ('x', 'yh'), 0, 0, tiled=True)  14.3 us
    pallas_call x2, Pallas kernels, product(): pl.pallas_call(kernel, out_shape=jax.ShapeDtypeStruct((count, width, cols...  11.1 us
  transfers between devices with their start and end apart: 23, of which 9 were waited for; matrix products, arithmetic and copies ran while one was open for 20% of the time, Pallas kernels for 4%

profile of v5, /device:TPU:1, one launch (start us, length us, event | category | flops | bytes accessed | tf_op | source)
XLA Modules:
  0.0 255.8 jit_solution(13759780306319730128)
XLA Ops:
  7.2 0.0 all-gather.5.cloned.1.call-start
  7.2 2.2 slice.24
  9.5 0.8 fusion.6
  10.3 2.5 collective-permute-start.1
  12.8 3.9 %collective-permute-start.2 = (bf16[1536,128]{1,0:T(8,128)(2,1)S(1)}, bf16[1536,128]{1,0:T(8,128)(2,1)S(1)}, u32[]{:S(2)}, u32[]{:S(2)}) collective-permute-start(bf16[1536,128]{1,0:T(8,128)(2,1)S(1)} %get-tuple-element.20.refs_0_), channel_id=1, source_target_pairs={{0,14},{2,0},{4,2},{6,4},{8,6},{10,8},{12,10},{14,12},{1,15},{3,1}... | collective-permute-start | bytes 1179656 | tf_op jit(solution)/shard_map/ppermute | solution.py:81
  16.7 1.3 convolution_reduce_fusion
  18.1 1.4 collective-permute-start
  19.5 1.5 collective-permute-done
  21.0 0.6 broadcast_in_dim.9
  21.6 5.3 %all-to-all-start = ((f32[8,1,1536]{2,1,0:T(1,128)}), f32[8,1,1536]{2,1,0:T(1,128)S(1)}, u32[]{:S(2)}, u32[]{:S(2)}) async-start(f32[8,1,1536]{2,1,0:T(1,128)} %broadcast_in_dim.9), calls=%async_computation | async-start | bytes 98304 | tf_op jit(solution)/shard_map/all_to_all | solution.py:26
  26.9 0.0 all-gather.7.cloned.1.call-start
  26.9 0.1 broadcast_bitcast_fusion
  27.0 7.6 %all-to-all-done = f32[8,1,1536]{2,1,0:T(1,128)S(1)} async-done(((f32[8,1,1536]{2,1,0:T(1,128)}), f32[8,1,1536]{2,1,0:T(1,128)S(1)}, u32[]{:S(2)}, u32[]{:S(2)}) %all-to-all-start) | async-done | bytes 49184 | tf_op jit(solution)/shard_map/all_to_all | solution.py:26
  34.7 0.1 multiply_multiply_fusion
  34.8 0.8 select_reduce_fusion.3
  35.6 1.3 pad_maximum_fusion.1
  36.9 17.3 %all_to_all.33 = f32[16,1,2]{2,1,0:T(1,128)S(1)} all-to-all(f32[16,1,2]{2,1,0:T(1,128)S(1)} %broadcast_in_dim.10), channel_id=1, replica_groups=mesh['x'=4,'yh'=2,'core'=2,'z'=8,'yl'=2] {'x','yh','core'}, dimensions={0} | all-to-all | bytes 256 | tf_op jit(solution)/shard_map/all_to_all | solution.py:26
  54.2 0.5 collective-permute-start.5
  54.7 0.3 collective-permute-start.3
  55.0 2.4 collective-permute-start.4
  57.4 0.6 compare_select_fusion.place_ref
  57.9 0.6 fusion.7
  59.9 15.3 %collective-permute-done.3.refs_3_ = bf16[1536,128]{1,0:T(8,128)(2,1)} collective-permute-done((bf16[1536,128]{1,0:T(8,128)(2,1)S(1)}, bf16[1536,128]{1,0:T(8,128)(2,1)}, u32[]{:S(2)}, u32[]{:S(2)}) %collective-permute-start.3) | collective-permute-done | bytes 393248 | tf_op jit(solution)/shard_map/ppermute | solution.py:81
  75.3 2.7 %collective-permute-start.7 = (bf16[1536,128]{1,0:T(8,128)(2,1)}, bf16[1536,128]{1,0:T(8,128)(2,1)S(1)}, u32[]{:S(2)}, u32[]{:S(2)}) collective-permute-start(bf16[1536,128]{1,0:T(8,128)(2,1)} %collective-permute-done.4.refs_4_), channel_id=1, source_target_pairs={{0,14},{2,0},{4,2},{6,4},{8,6},{10,8},{12,10},{14,12},{1,15},{3,1}... | collective-permute-start | bytes 1179656 | tf_op jit(solution)/shard_map/ppermute | solution.py:81
  78.0 0.7 add_divide_fusion
  78.6 0.1 select_reduce_fusion.4
  78.7 0.8 fusion.5
  79.5 16.3 %collective-permute-done.6.refs_5_ = bf16[1536,128]{1,0:T(8,128)(2,1)S(1)} collective-permute-done((bf16[1536,128]{1,0:T(8,128)(2,1)}, bf16[1536,128]{1,0:T(8,128)(2,1)S(1)}, u32[]{:S(2)}, u32[]{:S(2)}) %collective-permute-start.6) | collective-permute-done | bytes 393248 | tf_op jit(solution)/shard_map/ppermute | solution.py:81
  95.8 0.1 collective-permute-start.8
  96.0 2.7 %collective-permute-start.9 = (bf16[768,128]{1,0:T(8,128)(2,1)S(1)}, bf16[768,128]{1,0:T(8,128)(2,1)S(1)}, u32[]{:S(2)}, u32[]{:S(2)}) collective-permute-start(bf16[768,128]{1,0:T(8,128)(2,1)S(1)} %slice.29), channel_id=1, source_target_pairs={{0,14},{2,0},{4,2},{6,4},{8,6},{10,8},{12,10},{14,12},{1,15},{3,1}... | collective-permute-start | bytes 589832 | tf_op jit(solution)/shard_map/ppermute | solution.py:81
  98.7 4.0 %broadcast_select_fusion = (bf16[1536,512]{1,0:T(8,128)(2,1)}, bf16[1536,512]{1,0:T(8,128)(2,1)}) fusion(pred[]{:T(512)S(6)} %eq.19, bf16[1536,512]{1,0:T(8,128)(2,1)S(1)} %copy-done.1, f32[1536]{0:T(1024)S(1)} %get-tuple-element.17, bf16[1536,512]{1,0:T(8,128)(2,1)} %collective-permute-done.5), kind=kLoop, calls=%fused_computation.16 | loop fusion | flops 6291456 | bytes 6297601 | tf_op jit(solution)/shard_map/jit(_where)/select_n | solution.py:125
  102.7 4.9 %collective-permute-done.8.refs_7_ = bf16[768,128]{1,0:T(8,128)(2,1)S(1)} collective-permute-done((bf16[768,128]{1,0:T(8,128)(2,1)S(1)}, bf16[768,128]{1,0:T(8,128)(2,1)S(1)}, u32[]{:S(2)}, u32[]{:S(2)}) %collective-permute-start.8) | collective-permute-done | bytes 196640 | tf_op jit(solution)/shard_map/ppermute | solution.py:81
  107.6 0.7 copy-done.9
  108.3 0.7 copy-done.10
  109.0 5.5 %shard_map.78 = f32[8,128,512]{2,1,0:T(8,128)} custom-call(s32[8]{0:T(128)} %compare_select_fusion.place_ref, bf16[1536,128]{1,0:T(8,128)(2,1)} %copy-done.4, bf16[1536,128]{1,0:T(8,128)(2,1)} %copy-done.7, bf16[1536,128]{1,0:T(8,128)(2,1)} %copy-done.8, bf16[1536,128]{1,0:T(8,128)(2,1)} %collective-permute-done.3.refs_3_, ...), custom_call_target="tpu_custom_call" | custom-call | flops 1610612736 | bytes 6815744 | tf_op jit(solution)/shard_map/pallas_call | solution.py:45
  114.5 2.6 %collective-permute-start.10 = (f32[8,128,512]{2,1,0:T(8,128)}, f32[8,128,512]{2,1,0:T(8,128)}, u32[]{:S(2)}, u32[]{:S(2)}) collective-permute-start(f32[8,128,512]{2,1,0:T(8,128)} %shard_map.78), channel_id=1, source_target_pairs={{0,16},{16,0},{1,17},{17,1},{2,18},{18,2},{3,19},{19,3},{4,20},{20... | collective-permute-start | bytes 6291464 | tf_op jit(solution)/shard_map/ppermute | solution.py:144
  117.2 5.6 %shard_map.77 = f32[8,128,512]{2,1,0:T(8,128)} custom-call(s32[8]{0:T(128)} %compare_select_fusion.place_ref, bf16[1536,128]{1,0:T(8,128)(2,1)} %copy-done.4, bf16[1536,128]{1,0:T(8,128)(2,1)} %copy-done.7, bf16[1536,128]{1,0:T(8,128)(2,1)} %copy-done.8, bf16[1536,128]{1,0:T(8,128)(2,1)} %collective-permute-done.3.refs_3_, ...), custom_call_target="tpu_custom_call" | custom-call | flops 1610612736 | bytes 6815744 | tf_op jit(solution)/shard_map/pallas_call | solution.py:45
  122.7 3.7 %add_convert_fusion.2 = bf16[8,128,512]{2,1,0:T(8,128)(2,1)} fusion(f32[8,128,512]{2,1,0:T(8,128)} %shard_map.77, f32[8,128,512]{2,1,0:T(8,128)} %collective-permute-done.10), kind=kLoop, calls=%fused_computation.9 | loop fusion | flops 1048576 | bytes 5242880 | tf_op jit(solution)/shard_map/convert_element_type | solution.py:134
  126.5 7.8 %convolution_bitcast_fusion = f32[8,256,512]{1,2,0:T(8,128)} fusion(bf16[8,1536,256]{2,1,0:T(8,128)(2,1)} %bitcast.44, bf16[1536,512]{1,0:T(8,128)(2,1)S(1)} %copy-done.3), kind=kOutput, calls=%fused_computation.4 | convolution fusion | flops 3221225472 | bytes 12058624 | tf_op jit(solution)/shard_map/dot_general | solution.py:131
  134.3 4.2 %all-to-all-start.3 = ((bf16[8,128,512]{2,1,0:T(8,128)(2,1)}), bf16[8,128,512]{2,1,0:T(8,128)(2,1)}, u32[]{:S(2)}, u32[]{:S(2)}) async-start(bf16[8,128,512]{2,1,0:T(8,128)(2,1)} %add_convert_fusion.2), calls=%async_computation.3 | async-start | bytes 2097152 | tf_op jit(solution)/shard_map/all_to_all | solution.py:137
  138.5 17.9 %all-gather.7.cloned.1.call-done = bf16[12288,128]{1,0:T(8,128)(2,1)} async-done(((bf16[1536,128]{1,0:T(8,128)(2,1)}), bf16[12288,128]{1,0:T(8,128)(2,1)}) %all-gather.7.cloned.1.call-update) | async-done | bytes 3145744 | tf_op jit(solution)/shard_map/all_gather | solution.py:66
  156.4 5.6 %convolution_bitcast_fusion.2 = f32[8,128,512]{1,2,0:T(8,128)} fusion(bf16[8,1536,128]{2,1,0:T(8,128)(2,1)} %bitcast.46, bf16[1536,512]{1,0:T(8,128)(2,1)} %get-tuple-element.9.refs_9_), kind=kOutput, calls=%fused_computation.10 | convolution fusion | flops 1610612736 | bytes 6815744 | tf_op jit(solution)/shard_map/dot_general | solution.py:131
  162.0 1.2 collective-permute-start.14
  163.3 5.6 %convolution_bitcast_fusion.1 = f32[8,256,512]{1,2,0:T(8,128)S(1)} fusion(bf16[8,1536,256]{2,1,0:T(8,128)(2,1)} %bitcast.45, bf16[1536,512]{1,0:T(8,128)(2,1)S(1)} %copy-done.2), kind=kOutput, calls=%fused_computation.5 | convolution fusion | flops 3221225472 | bytes 12058624 | tf_op jit(solution)/shard_map/dot_general | solution.py:131
  168.9 4.1 %add_convert_fusion = bf16[8,256,512]{1,2,0:T(8,128)(2,1)} fusion(f32[8,256,512]{1,2,0:T(8,128)S(1)} %convolution_bitcast_fusion.1, f32[8,256,512]{1,2,0:T(8,128)} %collective-permute-done.11), kind=kLoop, calls=%fused_computation.1 | loop fusion | flops 2097152 | bytes 10485760 | tf_op jit(solution)/shard_map/convert_element_type | solution.py:134
  173.0 6.4 %all-to-all-start.2 = ((bf16[8,256,512]{1,2,0:T(8,128)(2,1)}), bf16[8,256,512]{1,2,0:T(8,128)(2,1)}, u32[]{:S(2)}, u32[]{:S(2)}) async-start(bf16[8,256,512]{1,2,0:T(8,128)(2,1)} %add_convert_fusion), calls=%async_computation.2 | async-start | bytes 4194304 | tf_op jit(solution)/shard_map/all_to_all | solution.py:137
  179.4 3.7 %convolution_bitcast_fusion.3 = f32[8,128,512]{1,2,0:T(8,128)S(1)} fusion(bf16[8,1536,128]{2,1,0:T(8,128)(2,1)} %bitcast.47, bf16[1536,512]{1,0:T(8,128)(2,1)S(1)} %copy-done.2), kind=kOutput, calls=%fused_computation.11 | convolution fusion | flops 1610612736 | bytes 6815744 | tf_op jit(solution)/shard_map/dot_general | solution.py:131
  183.2 2.8 %add_convert_fusion.1 = bf16[8,128,512]{1,2,0:T(8,128)(2,1)} fusion(f32[8,128,512]{1,2,0:T(8,128)S(1)} %convolution_bitcast_fusion.3, f32[8,128,512]{1,2,0:T(8,128)} %collective-permute-done.14), kind=kLoop, calls=%fused_computation.7 | loop fusion | flops 1048576 | bytes 5242880 | tf_op jit(solution)/shard_map/convert_element_type | solution.py:134
  185.9 24.8 %all-to-all-done.2 = bf16[8,256,512]{1,2,0:T(8,128)(2,1)} async-done(((bf16[8,256,512]{1,2,0:T(8,128)(2,1)}), bf16[8,256,512]{1,2,0:T(8,128)(2,1)}, u32[]{:S(2)}, u32[]{:S(2)}) %all-to-all-start.2) | async-done | bytes 2097184 | tf_op jit(solution)/shard_map/all_to_all | solution.py:137
  210.7 3.7 %all-to-all-start.4 = ((bf16[8,128,512]{1,2,0:T(8,128)(2,1)}), bf16[8,128,512]{1,2,0:T(8,128)(2,1)S(1)}, u32[]{:S(2)}, u32[]{:S(2)}) async-start(bf16[8,128,512]{1,2,0:T(8,128)(2,1)} %add_convert_fusion.1), calls=%async_computation.4 | async-start | bytes 2097152 | tf_op jit(solution)/shard_map/all_to_all | solution.py:137
  214.4 1.9 convert_reduce_fusion
  216.4 1.0 copy.18
  217.4 3.5 %collective-permute-start.12 = (f32[256,512]{1,0:T(8,128)}, f32[256,512]{1,0:T(8,128)S(1)}, u32[]{:S(2)}, u32[]{:S(2)}) collective-permute-start(f32[256,512]{1,0:T(8,128)} %copy.18), channel_id=1, source_target_pairs={{0,0},{1,16},{16,1},{17,17},{2,2},{3,18},{18,3},{19,19},{4,4},{5,2... | collective-permute-start | bytes 1572872 | tf_op jit(solution)/shard_map/ppermute | solution.py:140
  220.9 2.1 convert_reduce_fusion.2
  223.0 2.0 collective-permute-start.13
  225.0 5.0 %all-to-all-done.4 = bf16[8,128,512]{1,2,0:T(8,128)(2,1)S(1)} async-done(((bf16[8,128,512]{1,2,0:T(8,128)(2,1)}), bf16[8,128,512]{1,2,0:T(8,128)(2,1)S(1)}, u32[]{:S(2)}, u32[]{:S(2)}) %all-to-all-start.4) | async-done | bytes 1048608 | tf_op jit(solution)/shard_map/all_to_all | solution.py:137
  230.0 0.1 convert_reduce_fusion.1
  230.2 0.1 copy.19
  230.3 3.3 %collective-permute-start.15 = (f32[128,512]{1,0:T(8,128)S(1)}, f32[128,512]{1,0:T(8,128)S(1)}, u32[]{:S(2)}, u32[]{:S(2)}) collective-permute-start(f32[128,512]{1,0:T(8,128)S(1)} %copy.19), channel_id=1, source_target_pairs={{0,0},{1,16},{16,1},{17,17},{2,2},{3,18},{18,3},{19,19},{4,4},{5,2... | collective-permute-start | bytes 786440 | tf_op jit(solution)/shard_map/ppermute | solution.py:140
  233.6 0.7 fusion.8
  234.3 1.2 collective-permute-done.16
  235.5 10.9 %all_to_all.34 = f32[8,1,512]{2,1,0:T(1,128)S(1)} all-to-all(f32[8,1,512]{2,1,0:T(1,128)S(1)} %broadcast_in_dim.11), channel_id=1, replica_groups=mesh['x'=4,'yh'=2,'core'=2,'z'=8,'yl'=2] {'x','yh'}, dimensions={0} | all-to-all | bytes 32768 | tf_op jit(solution)/shard_map/all_to_all | solution.py:26
  246.3 0.6 reduce_sum.109
  246.9 2.0 pad_maximum_fusion
  (61 shorter events, 0.3 us)
Async XLA Ops:
  7.2 9.6 %copy-start = (f32[512]{0:T(512)S(1)}, f32[512]{0:T(512)}, u32[]{:S(2)}) copy-start(f32[512]{0:T(512)} %param.8) | copy-start | bytes 6148
  7.2 2.3 copy-start.1
  7.2 119.3 %all-gather.5.cloned.1.call-start = ((), (), s32[]{:S(2)}) async-start(), calls=%async_computation.6 | async-start | bytes 7077888 | tf_op jit(solution)/shard_map/all_gather | solution.py:65
  9.5 10.0 %copy-start.14 = (s32[1,12]{1,0:T(1,128)S(1)}, s32[1,12]{1,0:T(1,128)}, u32[]{:S(2)}) copy-start(s32[1,12]{1,0:T(1,128)} %param.10) | copy-start | bytes 148
  9.5 17.5 %copy-start.13 = (s32[1,1536]{1,0:T(1,128)S(1)}, s32[1,1536]{1,0:T(1,128)}, u32[]{:S(2)}) copy-start(s32[1,1536]{1,0:T(1,128)} %param.9) | copy-start | bytes 18436
  9.5 25.2 %copy-start.12 = (f32[1536]{0:T(1024)S(1)}, f32[1536]{0:T(1024)}, u32[]{:S(2)}) copy-start(f32[1536]{0:T(1024)} %param.7) | copy-start | bytes 18436
  9.5 47.9 %copy-start.15 = (s32[8]{0:T(128)S(1)}, s32[8]{0:T(128)}, u32[]{:S(2)}) copy-start(s32[8]{0:T(128)} %constant.33.clone) | copy-start | bytes 100
  10.3 92.3 %copy-start.4 = (bf16[1536,128]{1,0:T(8,128)(2,1)}, bf16[1536,128]{1,0:T(8,128)(2,1)S(1)}, u32[]{:S(2)}) copy-start(bf16[1536,128]{1,0:T(8,128)(2,1)S(1)} %get-tuple-element.20.refs_0_) | copy-start | bytes 1179652
  10.3 24.3 %collective-permute-start.1 = (bf16[1536,128]{1,0:T(8,128)(2,1)S(1)}, bf16[1536,128]{1,0:T(8,128)(2,1)S(1)}, u32[]{:S(2)}, u32[]{:S(2)}) collective-permute-start(bf16[1536,128]{1,0:T(8,128)(2,1)S(1)} %get-tuple-element.20.refs_0_), channel_id=1, source_target_pairs={{0,2},{2,4},{4,6},{6,8},{8,10},{10,12},{12,14},{14,0},{1,3},{3,5},... | collective-permute-start | bytes 1179656 | tf_op jit(solution)/shard_map/ppermute | solution.py:81
  12.8 21.9 %collective-permute-start.2 = (bf16[1536,128]{1,0:T(8,128)(2,1)S(1)}, bf16[1536,128]{1,0:T(8,128)(2,1)S(1)}, u32[]{:S(2)}, u32[]{:S(2)}) collective-permute-start(bf16[1536,128]{1,0:T(8,128)(2,1)S(1)} %get-tuple-element.20.refs_0_), channel_id=1, source_target_pairs={{0,14},{2,0},{4,2},{6,4},{8,6},{10,8},{12,10},{14,12},{1,15},{3,1}... | collective-permute-start | bytes 1179656 | tf_op jit(solution)/shard_map/ppermute | solution.py:81
  18.1 2.9 %collective-permute-start = (f32[1536]{0:T(1024)S(1)}, f32[1536]{0:T(1024)S(1)}, u32[]{:S(2)}, u32[]{:S(2)}) collective-permute-start(f32[1536]{0:T(1024)S(1)} %convolution_reduce_fusion), channel_id=1, source_target_pairs={{0,1},{1,0},{2,3},{3,2},{4,5},{5,4},{6,7},{7,6},{8,9},{9,8},{10,11... | collective-permute-start | bytes 18440 | tf_op jit(solution)/shard_map/ppermute | solution.py:94
  21.6 13.0 %all-to-all-start = ((f32[8,1,1536]{2,1,0:T(1,128)}), f32[8,1,1536]{2,1,0:T(1,128)S(1)}, u32[]{:S(2)}, u32[]{:S(2)}) async-start(f32[8,1,1536]{2,1,0:T(1,128)} %broadcast_in_dim.9), calls=%async_computation | async-start | bytes 98304 | tf_op jit(solution)/shard_map/all_to_all | solution.py:26
  26.9 129.5 %all-gather.7.cloned.1.call-start = ((), (), s32[]{:S(2)}) async-start(), calls=%async_computation.7 | async-start | bytes 3538944 | tf_op jit(solution)/shard_map/all_gather | solution.py:66
  34.7 25.3 %copy-start.11 = (f32[1536]{0:T(1024)}, f32[1536]{0:T(1024)S(1)}, u32[]{:S(2)}) copy-start(f32[1536]{0:T(1024)S(1)} %sub.3) | copy-start | bytes 18436
  34.7 68.0 %copy-start.7 = (bf16[1536,128]{1,0:T(8,128)(2,1)}, bf16[1536,128]{1,0:T(8,128)(2,1)S(1)}, u32[]{:S(2)}) copy-start(bf16[1536,128]{1,0:T(8,128)(2,1)S(1)} %collective-permute-done.1.refs_1_) | copy-start | bytes 1179652
  34.7 67.9 %copy-start.8 = (bf16[1536,128]{1,0:T(8,128)(2,1)}, bf16[1536,128]{1,0:T(8,128)(2,1)S(1)}, u32[]{:S(2)}) copy-start(bf16[1536,128]{1,0:T(8,128)(2,1)S(1)} %collective-permute-done.2.refs_2_) | copy-start | bytes 1179652
  54.2 44.5 %collective-permute-start.5 = (bf16[1536,512]{1,0:T(8,128)(2,1)S(1)}, bf16[1536,512]{1,0:T(8,128)(2,1)}, u32[]{:S(2)}, u32[]{:S(2)}) collective-permute-start(bf16[1536,512]{1,0:T(8,128)(2,1)S(1)} %copy-done.1), channel_id=1, source_target_pairs={{0,1},{1,0},{2,3},{3,2},{4,5},{5,4},{6,7},{7,6},{8,9},{9,8},{10,11... | collective-permute-start | bytes 4718600 | tf_op jit(solution)/shard_map/ppermute | solution.py:107
  54.7 20.6 %collective-permute-start.3 = (bf16[1536,128]{1,0:T(8,128)(2,1)S(1)}, bf16[1536,128]{1,0:T(8,128)(2,1)}, u32[]{:S(2)}, u32[]{:S(2)}) collective-permute-start(bf16[1536,128]{1,0:T(8,128)(2,1)S(1)} %collective-permute-done.1.refs_1_), channel_id=1, source_target_pairs={{0,2},{2,4},{4,6},{6,8},{8,10},{10,12},{12,14},{14,0},{1,3},{3,5},... | collective-permute-start | bytes 1179656 | tf_op jit(solution)/shard_map/ppermute | solution.py:81
  55.0 20.3 %collective-permute-start.4 = (bf16[1536,128]{1,0:T(8,128)(2,1)S(1)}, bf16[1536,128]{1,0:T(8,128)(2,1)}, u32[]{:S(2)}, u32[]{:S(2)}) collective-permute-start(bf16[1536,128]{1,0:T(8,128)(2,1)S(1)} %collective-permute-done.2.refs_2_), channel_id=1, source_target_pairs={{0,14},{2,0},{4,2},{6,4},{8,6},{10,8},{12,10},{14,12},{1,15},{3,1}... | collective-permute-start | bytes 1179656 | tf_op jit(solution)/shard_map/ppermute | solution.py:81
  75.3 20.5 %collective-permute-start.6 = (bf16[1536,128]{1,0:T(8,128)(2,1)}, bf16[1536,128]{1,0:T(8,128)(2,1)S(1)}, u32[]{:S(2)}, u32[]{:S(2)}) collective-permute-start(bf16[1536,128]{1,0:T(8,128)(2,1)} %collective-permute-done.3.refs_3_), channel_id=1, source_target_pairs={{0,2},{2,4},{4,6},{6,8},{8,10},{10,12},{12,14},{14,0},{1,3},{3,5},... | collective-permute-start | bytes 1179656 | tf_op jit(solution)/shard_map/ppermute | solution.py:81
  75.3 20.7 %collective-permute-start.7 = (bf16[1536,128]{1,0:T(8,128)(2,1)}, bf16[1536,128]{1,0:T(8,128)(2,1)S(1)}, u32[]{:S(2)}, u32[]{:S(2)}) collective-permute-start(bf16[1536,128]{1,0:T(8,128)(2,1)} %collective-permute-done.4.refs_4_), channel_id=1, source_target_pairs={{0,14},{2,0},{4,2},{6,4},{8,6},{10,8},{12,10},{14,12},{1,15},{3,1}... | collective-permute-start | bytes 1179656 | tf_op jit(solution)/shard_map/ppermute | solution.py:81
  95.8 6.8 %copy-start.5 = (bf16[1536,128]{1,0:T(8,128)(2,1)}, bf16[1536,128]{1,0:T(8,128)(2,1)S(1)}, u32[]{:S(2)}) copy-start(bf16[1536,128]{1,0:T(8,128)(2,1)S(1)} %collective-permute-done.6.refs_5_) | copy-start | bytes 1179652
  95.8 11.8 %collective-permute-start.8 = (bf16[768,128]{1,0:T(8,128)(2,1)S(1)}, bf16[768,128]{1,0:T(8,128)(2,1)S(1)}, u32[]{:S(2)}, u32[]{:S(2)}) collective-permute-start(bf16[768,128]{1,0:T(8,128)(2,1)S(1)} %slice.28), channel_id=1, source_target_pairs={{0,2},{2,4},{4,6},{6,8},{8,10},{10,12},{12,14},{14,0},{1,3},{3,5},... | collective-permute-start | bytes 589832 | tf_op jit(solution)/shard_map/ppermute | solution.py:81
  95.9 6.7 %copy-start.6 = (bf16[1536,128]{1,0:T(8,128)(2,1)}, bf16[1536,128]{1,0:T(8,128)(2,1)S(1)}, u32[]{:S(2)}) copy-start(bf16[1536,128]{1,0:T(8,128)(2,1)S(1)} %collective-permute-done.7.refs_6_) | copy-start | bytes 1179652
  96.0 12.3 %collective-permute-start.9 = (bf16[768,128]{1,0:T(8,128)(2,1)S(1)}, bf16[768,128]{1,0:T(8,128)(2,1)S(1)}, u32[]{:S(2)}, u32[]{:S(2)}) collective-permute-start(bf16[768,128]{1,0:T(8,128)(2,1)S(1)} %slice.29), channel_id=1, source_target_pairs={{0,14},{2,0},{4,2},{6,4},{8,6},{10,8},{12,10},{14,12},{1,15},{3,1}... | collective-permute-start | bytes 589832 | tf_op jit(solution)/shard_map/ppermute | solution.py:81
  107.6 0.7 copy-start.9
  108.3 0.7 copy-start.10
  114.5 8.2 %collective-permute-start.10 = (f32[8,128,512]{2,1,0:T(8,128)}, f32[8,128,512]{2,1,0:T(8,128)}, u32[]{:S(2)}, u32[]{:S(2)}) collective-permute-start(f32[8,128,512]{2,1,0:T(8,128)} %shard_map.78), channel_id=1, source_target_pairs={{0,16},{16,0},{1,17},{17,1},{2,18},{18,2},{3,19},{19,3},{4,20},{20... | collective-permute-start | bytes 6291464 | tf_op jit(solution)/shard_map/ppermute | solution.py:144
  122.7 3.8 %copy-start.3 = (bf16[1536,512]{1,0:T(8,128)(2,1)S(1)}, bf16[1536,512]{1,0:T(8,128)(2,1)}, u32[]{:S(2)}) copy-start(bf16[1536,512]{1,0:T(8,128)(2,1)} %get-tuple-element.9.refs_9_) | copy-start | bytes 4718596
  134.2 34.6 %collective-permute-start.11 = (f32[8,256,512]{1,2,0:T(8,128)}, f32[8,256,512]{1,2,0:T(8,128)}, u32[]{:S(2)}, u32[]{:S(2)}) collective-permute-start(f32[8,256,512]{1,2,0:T(8,128)} %convolution_bitcast_fusion), channel_id=1, source_target_pairs={{0,16},{16,0},{1,17},{17,1},{2,18},{18,2},{3,19},{19,3},{4,20},{20... | collective-permute-start | bytes 12582920 | tf_op jit(solution)/shard_map/ppermute | solution.py:144
  134.3 38.7 %all-to-all-start.3 = ((bf16[8,128,512]{2,1,0:T(8,128)(2,1)}), bf16[8,128,512]{2,1,0:T(8,128)(2,1)}, u32[]{:S(2)}, u32[]{:S(2)}) async-start(bf16[8,128,512]{2,1,0:T(8,128)(2,1)} %add_convert_fusion.2), calls=%async_computation.3 | async-start | bytes 2097152 | tf_op jit(solution)/shard_map/all_to_all | solution.py:137
  156.4 6.8 %copy-start.2 = (bf16[1536,512]{1,0:T(8,128)(2,1)S(1)}, bf16[1536,512]{1,0:T(8,128)(2,1)}, u32[]{:S(2)}) copy-start(bf16[1536,512]{1,0:T(8,128)(2,1)} %get-tuple-element.19.refs_9_) | copy-start | bytes 4718596
  162.0 21.1 %collective-permute-start.14 = (f32[8,128,512]{1,2,0:T(8,128)}, f32[8,128,512]{1,2,0:T(8,128)}, u32[]{:S(2)}, u32[]{:S(2)}) collective-permute-start(f32[8,128,512]{1,2,0:T(8,128)} %convolution_bitcast_fusion.2), channel_id=1, source_target_pairs={{0,16},{16,0},{1,17},{17,1},{2,18},{18,2},{3,19},{19,3},{4,20},{20... | collective-permute-start | bytes 6291464 | tf_op jit(solution)/shard_map/ppermute | solution.py:144
  173.0 37.8 %all-to-all-start.2 = ((bf16[8,256,512]{1,2,0:T(8,128)(2,1)}), bf16[8,256,512]{1,2,0:T(8,128)(2,1)}, u32[]{:S(2)}, u32[]{:S(2)}) async-start(bf16[8,256,512]{1,2,0:T(8,128)(2,1)} %add_convert_fusion), calls=%async_computation.2 | async-start | bytes 4194304 | tf_op jit(solution)/shard_map/all_to_all | solution.py:137
  210.7 19.3 %all-to-all-start.4 = ((bf16[8,128,512]{1,2,0:T(8,128)(2,1)}), bf16[8,128,512]{1,2,0:T(8,128)(2,1)S(1)}, u32[]{:S(2)}, u32[]{:S(2)}) async-start(bf16[8,128,512]{1,2,0:T(8,128)(2,1)} %add_convert_fusion.1), calls=%async_computation.4 | async-start | bytes 2097152 | tf_op jit(solution)/shard_map/all_to_all | solution.py:137
  217.4 29.6 %collective-permute-start.12 = (f32[256,512]{1,0:T(8,128)}, f32[256,512]{1,0:T(8,128)S(1)}, u32[]{:S(2)}, u32[]{:S(2)}) collective-permute-start(f32[256,512]{1,0:T(8,128)} %copy.18), channel_id=1, source_target_pairs={{0,0},{1,16},{16,1},{17,17},{2,2},{3,18},{18,3},{19,19},{4,4},{5,2... | collective-permute-start | bytes 1572872 | tf_op jit(solution)/shard_map/ppermute | solution.py:140
  223.0 24.0 %collective-permute-start.13 = (f32[128,512]{1,0:T(8,128)}, f32[128,512]{1,0:T(8,128)}, u32[]{:S(2)}, u32[]{:S(2)}) collective-permute-start(f32[128,512]{1,0:T(8,128)} %convert_reduce_fusion.2), channel_id=1, source_target_pairs={{0,0},{1,16},{16,1},{17,17},{2,2},{3,18},{18,3},{19,19},{4,4},{5,2... | collective-permute-start | bytes 786440 | tf_op jit(solution)/shard_map/ppermute | solution.py:140
  230.3 16.6 %collective-permute-start.15 = (f32[128,512]{1,0:T(8,128)S(1)}, f32[128,512]{1,0:T(8,128)S(1)}, u32[]{:S(2)}, u32[]{:S(2)}) collective-permute-start(f32[128,512]{1,0:T(8,128)S(1)} %copy.19), channel_id=1, source_target_pairs={{0,0},{1,16},{16,1},{17,17},{2,2},{3,18},{18,3},{19,19},{4,4},{5,2... | collective-permute-start | bytes 786440 | tf_op jit(solution)/shard_map/ppermute | solution.py:140
  234.3 1.2 collective-permute-start.16
Sparse Core Ops, SparseCore 0:
  9.8 99.8 all-gather.4
  117.3 39.0 all-gather.6
